TPU v7x, 32 devices: a whole 2x2x4 slice. The times are simulated.
32 devices in a mesh: mem: 8 (over y, x, core), col: 4 (over z).
Axes of the slice: x: 2, y: 2, z: 4, core: 2. Of those that a mesh axis runs over, the one named last changes fastest.
Arguments:
- background_trials: bfloat16 [256, 4, 32, 512], P('mem', None, None, 'col'), may hold values from -6 to 6
- region_active_tally: int32 [8, 16], P('mem', 'col'), may hold values from 256 to 2048, as said below
- sensed_component: int32 [8, 16, 2048], P('mem', 'col'), may hold values from 0 to 1919
- distance_bucket: int32 [8, 16, 2048], P('mem', 'col'), may hold values from 0 to 15
- sensor_readings: float32 [8, 16, 2048], P('mem', 'col'), may hold values from -6 to 6
- inverse_noise_variance: float32 [8, 16, 2048], P('mem', 'col'), may hold values from 0.25 to 4
- localization_factors: float32 [16], replicated, may hold values from 0.05 to 1
Outputs:
- analysis: bfloat16 [256, 4, 32, 512], P('mem', None, None, 'col')
Inputs may be any that keep to these rules, and one draw needn't show every extreme that they name: `region_active_tally`: observations of a patch fill its first slots; some patch has exactly 2048 live observations.
All inputs are finite; a program needn't handle non-finite values.
Results may differ from a plain program's by a relative error of at most 0.0063.
Values may be sent and summed in bfloat16 or wider, within the bound.
No kernel may reach another device: no remote copies, remote signals or barrier semaphores. Data moves between devices by JAX's collectives and lax.ppermute only.
A program may use at most 64 MiB of HBM per device.

v0:
```python
import jax
import jax.numpy as jnp
from jax import lax
from jax.sharding import PartitionSpec as P

SECTOR_SPAN = 32
REACH_MARGIN = 4
ITERS = 4


inflation = 1.1
obs_block = 128


def padded(block, sides, width):
    for axis, dim in sides:
        count = lax.axis_size(axis)
        forward = [(i, i + 1) for i in range(count - 1)]
        backward = [(target, source) for source, target in forward]
        low = lax.ppermute(
            lax.slice_in_dim(block, block.shape[dim] - width, None, axis=dim), axis, forward
        )
        high = lax.ppermute(lax.slice_in_dim(block, 0, width, axis=dim), axis, backward)
        block = jnp.concatenate([low, block, high], axis=dim)
    return block


def lookup(class_ids, weight_table):
    table_slots = jnp.arange(weight_table.shape[0], dtype=jnp.int32)
    return jnp.sum(jnp.where(class_ids[..., None] == table_slots, weight_table, 0.0), axis=-1)


def observe(
    anomaly_flat, average_flat, cell_ids, class_ids, values, inv_var, is_live, weight_table
):
    observed = jnp.take_along_axis(anomaly_flat, cell_ids[:, None, :], axis=2)
    innovation = values - jnp.take_along_axis(average_flat, cell_ids, axis=1)
    weight = jnp.where(is_live, inv_var * lookup(class_ids, weight_table), 0.0)
    scaled = (observed.astype(jnp.float32) * weight[:, None, :]).astype(jnp.bfloat16)
    gram_part = jnp.einsum("qkm,qjm->qkj", scaled, observed, preferred_element_type=jnp.float32)
    forcing_part = jnp.einsum(
        "qkm,qm->qk", scaled.astype(jnp.float32), innovation, precision=lax.Precision.HIGHEST
    )
    return (gram_part, forcing_part)


def local(
    background_trials,
    region_active_tally,
    sensed_component,
    distance_bucket,
    sensor_readings,
    inverse_noise_variance,
    localization_factors,
):
    local_region_tile = lax.all_to_all(
        background_trials, "mem", split_axis=2, concat_axis=0, tiled=True
    )
    enlarged_piece = padded(local_region_tile, (("mem", 2), ("col", 3)), REACH_MARGIN)
    trial_flattened = enlarged_piece.shape[0]
    physical_quantity_stack = enlarged_piece.shape[1]
    tile_height = enlarged_piece.shape[2] - 2 * REACH_MARGIN
    tile_width = enlarged_piece.shape[3] - 2 * REACH_MARGIN
    patches = tile_width // SECTOR_SPAN
    frame_breadth = SECTOR_SPAN + 2 * REACH_MARGIN
    unit_weights = jnp.ones((trial_flattened,), jnp.bfloat16)
    predicted_average = (
        lax.dot_general(
            unit_weights,
            enlarged_piece,
            (((0,), (0,)), ((), ())),
            preferred_element_type=jnp.float32,
        )
        / trial_flattened
    )
    deviation_matrix = (enlarged_piece.astype(jnp.float32) - predicted_average).astype(jnp.bfloat16)
    anomaly_flat = jnp.stack(
        [
            deviation_matrix[
                :, :, :, sector_index * SECTOR_SPAN : sector_index * SECTOR_SPAN + frame_breadth
            ]
            for sector_index in range(patches)
        ]
    ).reshape(patches, trial_flattened, -1)
    average_flat = jnp.stack(
        [
            predicted_average[
                :, :, sector_index * SECTOR_SPAN : sector_index * SECTOR_SPAN + frame_breadth
            ]
            for sector_index in range(patches)
        ]
    ).reshape(patches, -1)
    counts = region_active_tally.reshape(patches)
    cell_ids = sensed_component.reshape(patches, -1)
    class_ids = distance_bucket.reshape(patches, -1)
    values = sensor_readings.reshape(patches, -1)
    inv_vars = inverse_noise_variance.reshape(patches, -1)
    order_ids = jnp.broadcast_to(jnp.arange(cell_ids.shape[1], dtype=jnp.int32), cell_ids.shape)
    rounds = (jnp.max(counts) + obs_block - 1) // obs_block

    def one_round(round_id, partial_sums):
        block_start = round_id * obs_block

        def take_block(source):
            return lax.dynamic_slice_in_dim(source, block_start, obs_block, 1)

        gram_part, forcing_part = observe(
            anomaly_flat,
            average_flat,
            take_block(cell_ids),
            take_block(class_ids),
            take_block(values),
            take_block(inv_vars),
            take_block(order_ids) < counts[:, None],
            localization_factors,
        )
        return (partial_sums[0] + gram_part, partial_sums[1] + forcing_part)

    initial = (
        jnp.zeros((patches, trial_flattened, trial_flattened), jnp.float32),
        jnp.zeros((patches, trial_flattened), jnp.float32),
    )
    gram_sum, forcing = lax.fori_loop(0, rounds, one_round, initial)
    identity = jnp.eye(trial_flattened, dtype=jnp.float32)
    gram_sum = gram_sum + (trial_flattened - 1) / inflation * identity
    norm_scale = jnp.sqrt(jnp.sum(gram_sum * gram_sum, axis=(1, 2)))
    iterate = gram_sum / norm_scale[:, None, None]
    inverse_root = jnp.broadcast_to(identity, iterate.shape)
    for sweep_id in range(ITERS):
        factor = 1.5 * identity - 0.5 * jnp.einsum(
            "qij,qjk->qik", inverse_root, iterate, precision=lax.Precision.HIGHEST
        )
        if sweep_id + 1 < ITERS:
            iterate = jnp.einsum("qij,qjk->qik", iterate, factor, precision=lax.Precision.HIGHEST)
        inverse_root = jnp.einsum(
            "qij,qjk->qik", factor, inverse_root, precision=lax.Precision.HIGHEST
        )
    partial_shift = jnp.einsum("qij,qj->qi", inverse_root, forcing, precision=lax.Precision.HIGHEST)
    mean_shift = (
        jnp.einsum("qij,qj->qi", inverse_root, partial_shift, precision=lax.Precision.HIGHEST)
        / norm_scale[:, None]
    )
    spread_scale = jnp.sqrt((trial_flattened - 1.0) / norm_scale)
    transform = (spread_scale[:, None, None] * inverse_root + mean_shift[:, :, None]).astype(
        jnp.bfloat16
    )
    own_anomaly = deviation_matrix[
        :, :, REACH_MARGIN : REACH_MARGIN + tile_height, REACH_MARGIN : REACH_MARGIN + tile_width
    ].reshape(trial_flattened, physical_quantity_stack, tile_height, patches, SECTOR_SPAN)
    inner_midpoint = predicted_average[
        :, REACH_MARGIN : REACH_MARGIN + tile_height, REACH_MARGIN : REACH_MARGIN + tile_width
    ].reshape(physical_quantity_stack, tile_height, patches, SECTOR_SPAN)
    analysed = (
        jnp.einsum("kstqp,qkj->jstqp", own_anomaly, transform, preferred_element_type=jnp.float32)
        + inner_midpoint[None]
    )
    analysed = analysed.astype(jnp.bfloat16).reshape(
        trial_flattened, physical_quantity_stack, tile_height, tile_width
    )
    return lax.all_to_all(analysed, "mem", split_axis=0, concat_axis=2, tiled=True)


def solution(mesh):
    placed = (
        P("mem", None, None, "col"),
        P("mem", "col"),
        P("mem", "col", None),
        P("mem", "col", None),
        P("mem", "col", None),
        P("mem", "col", None),
        P(),
    )
    return jax.shard_map(
        local, mesh=mesh, in_specs=placed, out_specs=P("mem", None, None, "col"), check_vma=False
    )
```

profile of v0, /device:TPU:0, one launch (start us, length us, event | category | flops | bytes accessed | tf_op | source)
XLA Modules:
  0.0 388.5 jit_solution(7699056529408383022)
XLA Ops:
  1.9 20.3 %all_to_all.36 = bf16[32,4,32,128]{3,0,1,2:T(8,128)(2,1)S(1)} all-to-all(bf16[32,4,32,128]{3,0,1,2:T(8,128)(2,1)S(1)} %copy.56), channel_id=1, replica_groups=mesh['mem'=8,'col'=4] {'mem'}, dimensions={2} | all-to-all | bytes 2097152 | tf_op jit(solution)/shard_map/all_to_all | solution.py:56
  30.4 3.0 fusion.34
  33.4 3.2 copy.59
  36.6 4.1 %collective-permute-start.2 = (bf16[256,4,12,4]{0,3,2,1:T(4,128)(2,1)S(1)}, bf16[256,4,12,4]{0,3,2,1:T(4,128)(2,1)}, u32[]{:S(2)}, u32[]{:S(2)}) collective-permute-start(bf16[256,4,12,4]{0,3,2,1:T(4,128)(2,1)S(1)} %copy.59), channel_id=1, source_target_pairs={{0,1},{1,2},{2,3},{4,5},{5,6},{6,7},{8,9},{9,10},{10,11},{12,13},{... | collective-permute-start | bytes 294920 | tf_op jit(solution)/shard_map/ppermute | solution.py:20
  45.1 2.6 copy.61
  49.7 3.6 copy.62
  53.3 7.1 %fusion.29 = f32[1,4,12,136]{3,0,2,1:T(1,128)S(1)} fusion(bf16[256,4,12,4]{3,0,2,1:T(8,128)(2,1)} %copy.62, bf16[256,4,4,128]{3,0,2,1:T(8,128)(2,1)} %copy-done.3, bf16[256,4,4,128]{3,0,2,1:T(8,128)(2,1)} %bitcast.95, bf16[256,4,4,128]{3,0,2,1:T(8,128)(2,1)} %copy-done.2, bf16[256,4,12,4]{3,0,2,1:T(8,128)(2,1)S(1)} %copy.61), kind=kOutput, calls=%fused_computation.60 | convolution fusion | flops 20054016 | bytes 3368448 | tf_op jit(solution)/shard_map/dot_general | solution.py:68
  63.6 8.0 %subtract_convert_fusion = bf16[256,4,12,136]{3,0,2,1:T(8,128)(2,1)S(1)} fusion(f32[4,12,136]{2,1,0:T(8,128)S(1)} %bitcast_multiply_fusion, bf16[256,4,12,4]{3,0,2,1:T(8,128)(2,1)} %copy.62, bf16[256,4,4,128]{3,0,2,1:T(8,128)(2,1)} %copy-done.3, bf16[256,4,4,128]{3,0,2,1:T(8,128)(2,1)} %bitcast.96, bf16[256,4,4,128]{3,0,2,1:T(8,128)(2,1)} %copy-done.2, ...), kind=kLoop, calls=%fused_computation.24 | loop fusion | flops 20054016 | bytes 6710784 | tf_op jit(solution)/shard_map/convert_element_type | solution.py:76
  71.6 5.4 %fusion.33 = (bf16[256,4,12,40]{3,0,2,1:T(8,128)(2,1)}, bf16[256,4,12,40]{3,0,2,1:T(8,128)(2,1)S(1)}, bf16[256,4,12,40]{3,0,2,1:T(8,128)(2,1)}, bf16[256,4,12,40]{3,0,2,1:T(8,128)(2,1)}) fusion(bf16[256,4,12,136]{3,0,2,1:T(8,128)(2,1)S(1)} %subtract_convert_fusion), kind=kLoop, calls=%fused_computation.65 | loop fusion | bytes 7864320 | tf_op jit(solution)/shard_map/slice | solution.py:79
  77.0 4.1 %copy.63 = bf16[256,4,12,40]{0,3,2,1:T(8,128)(2,1)} copy(bf16[256,4,12,40]{3,0,2,1:T(8,128)(2,1)} %get-tuple-element.105) | data formatting | bytes 1966080 | tf_op jit(solution)/shard_map/slice | solution.py:79
  81.1 4.1 %copy.64 = bf16[256,4,12,40]{0,3,2,1:T(8,128)(2,1)} copy(bf16[256,4,12,40]{3,0,2,1:T(8,128)(2,1)} %get-tuple-element.108) | data formatting | bytes 1966080 | tf_op jit(solution)/shard_map/slice | solution.py:79
  85.2 4.1 %copy.65 = bf16[256,4,12,40]{0,3,2,1:T(8,128)(2,1)} copy(bf16[256,4,12,40]{3,0,2,1:T(8,128)(2,1)} %get-tuple-element.107) | data formatting | bytes 1966080 | tf_op jit(solution)/shard_map/slice | solution.py:79
  89.2 2.2 copy.66
  91.5 3.7 pad_maximum_fusion.1
  95.3 117.3 %while.12 = (s32[]{:T(128)}, f32[4,256,256]{2,1,0:T(8,128)S(1)}, f32[4,256]{1,0:T(4,128)S(1)}, s32[]{:T(128)}, s32[4,2048]{1,0:T(4,128)}, /*index=5*/bf16[4,256,...) while((s32[]{:T(128)}, f32[4,256,256]{2,1,0:T(8,128)S(1)}, ...), condition=%wide.region_3.4_spmd, body=%wide.region_1.3_spmd.sunk | while | flops 70158344 | bytes 3735335 | solution.py:123
  96.1 4.8 %gather_fusion = f32[512]{0:T(512)S(1)} fusion(f32[4,1920]{1,0:T(4,128)S(1)} %get-tuple-element.251, s32[512]{0:T(512)S(1)} %fusion.67), kind=kCustom, calls=%fused_computation.1.clone.1 | custom fusion | bytes 8192 | tf_op jit(solution)/shard_map/while/body/jit(take_along_axis)/gather | solution.py:37
  102.5 6.6 %gather_fusion.1 = bf16[512,256]{1,0:T(8,128)(2,1)S(1)} fusion(bf16[4,256,1920]{1,2,0:T(8,128)(2,1)} %get-tuple-element.244, s32[512]{0:T(512)S(1)} %fusion.67), kind=kCustom, calls=%fused_computation.clone.1 | custom fusion | bytes 528384 | tf_op jit(solution)/shard_map/while/body/jit(take_along_axis)/gather | solution.py:36
  110.8 4.8 %gather_fusion = f32[512]{0:T(512)S(1)} fusion(f32[4,1920]{1,0:T(4,128)S(1)} %get-tuple-element.251, s32[512]{0:T(512)S(1)} %fusion.67), kind=kCustom, calls=%fused_computation.1.clone.1 | custom fusion | bytes 8192 | tf_op jit(solution)/shard_map/while/body/jit(take_along_axis)/gather | solution.py:37
  117.2 6.6 %gather_fusion.1 = bf16[512,256]{1,0:T(8,128)(2,1)S(1)} fusion(bf16[4,256,1920]{1,2,0:T(8,128)(2,1)} %get-tuple-element.244, s32[512]{0:T(512)S(1)} %fusion.67), kind=kCustom, calls=%fused_computation.clone.1 | custom fusion | bytes 528384 | tf_op jit(solution)/shard_map/while/body/jit(take_along_axis)/gather | solution.py:36
  125.4 4.8 %gather_fusion = f32[512]{0:T(512)S(1)} fusion(f32[4,1920]{1,0:T(4,128)S(1)} %get-tuple-element.251, s32[512]{0:T(512)S(1)} %fusion.67), kind=kCustom, calls=%fused_computation.1.clone.1 | custom fusion | bytes 8192 | tf_op jit(solution)/shard_map/while/body/jit(take_along_axis)/gather | solution.py:37
  131.8 6.6 %gather_fusion.1 = bf16[512,256]{1,0:T(8,128)(2,1)S(1)} fusion(bf16[4,256,1920]{1,2,0:T(8,128)(2,1)} %get-tuple-element.244, s32[512]{0:T(512)S(1)} %fusion.67), kind=kCustom, calls=%fused_computation.clone.1 | custom fusion | bytes 528384 | tf_op jit(solution)/shard_map/while/body/jit(take_along_axis)/gather | solution.py:36
  140.0 4.8 %gather_fusion = f32[512]{0:T(512)S(1)} fusion(f32[4,1920]{1,0:T(4,128)S(1)} %get-tuple-element.251, s32[512]{0:T(512)S(1)} %fusion.67), kind=kCustom, calls=%fused_computation.1.clone.1 | custom fusion | bytes 8192 | tf_op jit(solution)/shard_map/while/body/jit(take_along_axis)/gather | solution.py:37
  146.4 6.6 %gather_fusion.1 = bf16[512,256]{1,0:T(8,128)(2,1)S(1)} fusion(bf16[4,256,1920]{1,2,0:T(8,128)(2,1)} %get-tuple-element.244, s32[512]{0:T(512)S(1)} %fusion.67), kind=kCustom, calls=%fused_computation.clone.1 | custom fusion | bytes 528384 | tf_op jit(solution)/shard_map/while/body/jit(take_along_axis)/gather | solution.py:36
  154.6 4.8 %gather_fusion = f32[512]{0:T(512)S(1)} fusion(f32[4,1920]{1,0:T(4,128)S(1)} %get-tuple-element.251, s32[512]{0:T(512)S(1)} %fusion.67), kind=kCustom, calls=%fused_computation.1.clone.1 | custom fusion | bytes 8192 | tf_op jit(solution)/shard_map/while/body/jit(take_along_axis)/gather | solution.py:37
  161.0 6.6 %gather_fusion.1 = bf16[512,256]{1,0:T(8,128)(2,1)S(1)} fusion(bf16[4,256,1920]{1,2,0:T(8,128)(2,1)} %get-tuple-element.244, s32[512]{0:T(512)S(1)} %fusion.67), kind=kCustom, calls=%fused_computation.clone.1 | custom fusion | bytes 528384 | tf_op jit(solution)/shard_map/while/body/jit(take_along_axis)/gather | solution.py:36
  169.3 4.8 %gather_fusion = f32[512]{0:T(512)S(1)} fusion(f32[4,1920]{1,0:T(4,128)S(1)} %get-tuple-element.251, s32[512]{0:T(512)S(1)} %fusion.67), kind=kCustom, calls=%fused_computation.1.clone.1 | custom fusion | bytes 8192 | tf_op jit(solution)/shard_map/while/body/jit(take_along_axis)/gather | solution.py:37
  175.7 6.6 %gather_fusion.1 = bf16[512,256]{1,0:T(8,128)(2,1)S(1)} fusion(bf16[4,256,1920]{1,2,0:T(8,128)(2,1)} %get-tuple-element.244, s32[512]{0:T(512)S(1)} %fusion.67), kind=kCustom, calls=%fused_computation.clone.1 | custom fusion | bytes 528384 | tf_op jit(solution)/shard_map/while/body/jit(take_along_axis)/gather | solution.py:36
  183.9 4.8 %gather_fusion = f32[512]{0:T(512)S(1)} fusion(f32[4,1920]{1,0:T(4,128)S(1)} %get-tuple-element.251, s32[512]{0:T(512)S(1)} %fusion.67), kind=kCustom, calls=%fused_computation.1.clone.1 | custom fusion | bytes 8192 | tf_op jit(solution)/shard_map/while/body/jit(take_along_axis)/gather | solution.py:37
  190.3 6.6 %gather_fusion.1 = bf16[512,256]{1,0:T(8,128)(2,1)S(1)} fusion(bf16[4,256,1920]{1,2,0:T(8,128)(2,1)} %get-tuple-element.244, s32[512]{0:T(512)S(1)} %fusion.67), kind=kCustom, calls=%fused_computation.clone.1 | custom fusion | bytes 528384 | tf_op jit(solution)/shard_map/while/body/jit(take_along_axis)/gather | solution.py:36
  198.5 4.8 %gather_fusion = f32[512]{0:T(512)S(1)} fusion(f32[4,1920]{1,0:T(4,128)S(1)} %get-tuple-element.251, s32[512]{0:T(512)S(1)} %fusion.67), kind=kCustom, calls=%fused_computation.1.clone.1 | custom fusion | bytes 8192 | tf_op jit(solution)/shard_map/while/body/jit(take_along_axis)/gather | solution.py:37
  204.9 6.6 %gather_fusion.1 = bf16[512,256]{1,0:T(8,128)(2,1)S(1)} fusion(bf16[4,256,1920]{1,2,0:T(8,128)(2,1)} %get-tuple-element.244, s32[512]{0:T(512)S(1)} %fusion.67), kind=kCustom, calls=%fused_computation.clone.1 | custom fusion | bytes 528384 | tf_op jit(solution)/shard_map/while/body/jit(take_along_axis)/gather | solution.py:36
  232.6 154.1 %all_to_all.37 = bf16[256,4,4,128]{3,2,1,0:T(4,128)(2,1)S(1)} all-to-all(bf16[256,4,4,128]{3,2,1,0:T(4,128)(2,1)S(1)} %copy.71), channel_id=1, replica_groups=mesh['mem'=8,'col'=4] {'mem'}, dimensions={0} | all-to-all | bytes 2097152 | tf_op jit(solution)/shard_map/all_to_all | solution.py:160
  (136 shorter events, 65.7 us)
Async XLA Ops:
  0.0 25.0 %copy-start.7 = (s32[1,4]{1,0:T(1,128)S(1)}, s32[1,4]{1,0:T(1,128)}, u32[]{:S(2)}) copy-start(s32[1,4]{1,0:T(1,128)} %param.10) | copy-start | bytes 52
  22.4 6.7 %copy-start.1 = (bf16[8,32,4,4,128]{4,1,0,3,2:T(8,128)(2,1)}, bf16[8,32,4,4,128]{4,1,0,3,2:T(8,128)(2,1)S(1)}, u32[]{:S(2)}) copy-start(bf16[8,32,4,4,128]{4,1,0,3,2:T(8,128)(2,1)S(1)} %copy.58) | copy-start | bytes 3145732
  22.4 4.7 %collective-permute-start = (bf16[256,4,4,128]{3,0,2,1:T(8,128)(2,1)S(1)}, bf16[256,4,4,128]{3,0,2,1:T(8,128)(2,1)S(1)}, u32[]{:S(2)}, u32[]{:S(2)}) collective-permute-start(bf16[256,4,4,128]{3,0,2,1:T(8,128)(2,1)S(1)} %bitcast.92), channel_id=1, source_target_pairs={{0,4},{4,8},{8,12},{12,16},{16,20},{20,24},{24,28},{1,5},{5,9},{9,... | collective-permute-start | bytes 3145736 | tf_op jit(solution)/shard_map/ppermute | solution.py:20
  23.7 5.3 %collective-permute-start.1 = (bf16[256,4,4,128]{3,0,2,1:T(8,128)(2,1)S(1)}, bf16[256,4,4,128]{3,0,2,1:T(8,128)(2,1)S(1)}, u32[]{:S(2)}, u32[]{:S(2)}) collective-permute-start(bf16[256,4,4,128]{3,0,2,1:T(8,128)(2,1)S(1)} %bitcast.93), channel_id=1, source_target_pairs={{4,0},{8,4},{12,8},{16,12},{20,16},{24,20},{28,24},{5,1},{9,5},{13... | collective-permute-start | bytes 3145736 | tf_op jit(solution)/shard_map/ppermute | solution.py:23
  27.1 1.9 copy-start.2
  29.0 1.0 copy-start.3
  36.6 8.5 %collective-permute-start.2 = (bf16[256,4,12,4]{0,3,2,1:T(4,128)(2,1)S(1)}, bf16[256,4,12,4]{0,3,2,1:T(4,128)(2,1)}, u32[]{:S(2)}, u32[]{:S(2)}) collective-permute-start(bf16[256,4,12,4]{0,3,2,1:T(4,128)(2,1)S(1)} %copy.59), channel_id=1, source_target_pairs={{0,1},{1,2},{2,3},{4,5},{5,6},{6,7},{8,9},{9,10},{10,11},{12,13},{... | collective-permute-start | bytes 294920 | tf_op jit(solution)/shard_map/ppermute | solution.py:20
  42.9 6.8 %collective-permute-start.3 = (bf16[256,4,12,4]{0,3,2,1:T(4,128)(2,1)}, bf16[256,4,12,4]{0,3,2,1:T(4,128)(2,1)}, u32[]{:S(2)}, u32[]{:S(2)}) collective-permute-start(bf16[256,4,12,4]{0,3,2,1:T(4,128)(2,1)} %copy.60), channel_id=1, source_target_pairs={{1,0},{2,1},{3,2},{5,4},{6,5},{7,6},{9,8},{10,9},{11,10},{13,12},{... | collective-permute-start | bytes 294920 | tf_op jit(solution)/shard_map/ppermute | solution.py:23
  71.6 5.4 %copy-start = (bf16[256,4,12,136]{3,0,2,1:T(8,128)(2,1)}, bf16[256,4,12,136]{3,0,2,1:T(8,128)(2,1)S(1)}, u32[]{:S(2)}) copy-start(bf16[256,4,12,136]{3,0,2,1:T(8,128)(2,1)S(1)} %subtract_convert_fusion) | copy-start | bytes 10027012
  85.2 6.3 %copy-start.6 = (f32[1,1920]{1,0:T(1,128)S(1)}, f32[1,1920]{1,0:T(1,128)}, u32[]{:S(2)}) copy-start(f32[1,1920]{1,0:T(1,128)} %stack.37) | copy-start | bytes 23044
  91.5 3.8 copy-start.8
  91.5 3.8 copy-start.9
  95.3 117.3 %copy-start.4 = (f32[256,256]{1,0:T(8,128)S(1)}, f32[256,256]{1,0:T(8,128)}, u32[]{:S(2)}) copy-start(f32[256,256]{1,0:T(8,128)} %get-tuple-element.118) | copy-start | bytes 786436
  95.3 117.6 %copy-start.5 = (f32[256,256]{1,0:T(8,128)S(1)}, f32[256,256]{1,0:T(8,128)}, u32[]{:S(2)}) copy-start(f32[256,256]{1,0:T(8,128)} %fusion.22) | copy-start | bytes 786436
where the time goes:
time: 391 us; the launch traced here: 389 us
  blocking collectives  174 us (45%)
  local copies, waits for them, and re-layouts  145 us (37%)
  matrix products  28.2 us (7%)
  other arithmetic  27.2 us (7%)
  starting transfers between devices  8.24 us (2%)
  waiting for transfers between devices  3.97 us (1%)
    all_to_all x1, blocking collectives, local(): lax.all_to_all(analysed, 'mem', split_axis=0, concat_axis=2, tiled=True)  154 us
    gather x16, local copies, waits for them, and re-layouts, observe(): observed = jnp.take_along_axis(anomaly_flat, cell_ids[:, None, :], axis=2)  54.3 us
    gather x8, local copies, waits for them, and re-layouts, observe(): innovation = values - jnp.take_along_axis(average_flat, cell_ids, axis=1)  38.7 us
    all_to_all x1, blocking collectives, local(): lax.all_to_all(background_trials, 'mem', split_axis=2, concat_axis=0, til...  20.3 us
    slice x5, local copies, waits for them, and re-layouts, local(): deviation_matrix[:, :, :, sector_index * SECTOR_SPAN:sector_index * SECTO...  19.8 us
    convert_element_type x1, other arithmetic, local(): (enlarged_piece.astype(jnp.float32) - predicted_average).astype(jnp.bfloa...  8.04 us
  transfers between devices with their start and end apart: 4, of which 2 were waited for; matrix products, arithmetic and copies ran while one was open for 2% of the time, Pallas kernels for 0%

commit v1 on v0

v1 whole, which is shorter than its diff:
```python
import functools
import jax
import jax.numpy as jnp
from jax import lax
from jax.experimental import pallas as pl
from jax.experimental.pallas import tpu as pltpu
from jax.sharding import PartitionSpec as P

DEPTH = 4
SPAN = 32
MARGIN = 4
ITERS = 4
LANES = 128
MAP_ROWS = 16
INFLATION = 1.1

f32 = jnp.float32
bf16 = jnp.bfloat16
i32 = jnp.int32
VMEM = pl.BlockSpec(memory_space=pltpu.VMEM)
SMEM = pl.BlockSpec(memory_space=pltpu.SMEM)
PARAMS = pltpu.CompilerParams(vmem_limit_bytes=24 * 1024 * 1024)


def iota(shape, dim):
    return lax.broadcasted_iota(i32, shape, dim)


def dot(a, b):
    return jnp.dot(a, b, preferred_element_type=f32)


def one_hot(condition):
    return jnp.where(condition, 1.0, 0.0).astype(bf16)


class Plan:
    def __init__(self, x_shape, count, states):
        self.members, self.states, self.rows, self.cols = x_shape
        self.count = count
        self.total = self.members * count
        self.patches = self.cols // SPAN
        self.bands = self.rows // DEPTH
        self.groups = self.bands // self.patches
        chips = count // 2
        if count % 2 == 0 and chips % self.patches == 0:
            self.place = [
                (2 * (i // 2 // self.patches) + i % 2, i // 2 % self.patches) for i in range(count)
            ]
        else:
            self.place = [(i // self.patches, i % self.patches) for i in range(count)]
        self.slot_bands = self.patches + min(2, self.groups - 1) if self.groups > 1 else self.patches
        self.full = self.slot_bands == self.patches + 2
        self.per_band = self.states + 1
        self.field = self.slot_bands * self.per_band
        self.map_groups = 4 * MAP_ROWS // self.members
        self.slot = self.field + self.map_groups
        self.index_of = {p: i for i, p in enumerate(self.place)}

    def first_band(self, group):
        low = self.patches * group - 1
        return low if self.full else max(low, 0)

    def band_slots(self, band):
        return [
            (g, band - self.first_band(g))
            for g in range(self.groups)
            if 0 <= band - self.first_band(g) < self.slot_bands
        ]


def side_source(lane, column, cols):
    eighth = lane % (2 * MARGIN)
    low = column * SPAN - MARGIN + eighth
    high = column * SPAN + SPAN + eighth - MARGIN
    return jnp.where(eighth < MARGIN, low, high)


def pack_kernel(plan, x_ref, buf_ref, up_ref, down_ref, turned, q_ref, side_ref):
    half = 16
    rows, cols = plan.rows, plan.cols
    span = half * rows
    r = iota((span, span), 0)
    k = iota((span, span), 1)
    perm = one_hot((r % half == k // rows) & (r // half == k % rows))
    for s in range(plan.states):
        for h in range(plan.members // half):
            piece = x_ref[h * half : (h + 1) * half, s].reshape(span, cols)
            turned[s, :, h * half : (h + 1) * half, :] = (
                dot(perm, piece).astype(bf16).reshape(rows, half, cols)
            )
    wide = DEPTH * cols
    r = iota((wide, wide), 0)
    k = iota((wide, wide), 1)
    q_ref[...] = one_hot(
        (r // cols == (k % LANES) // SPAN) & (r % cols == (k // LANES) * SPAN + k % SPAN)
    )
    n_side = (plan.patches + 2) * LANES
    col = iota((cols, n_side), 0)
    out = iota((cols, n_side), 1)
    column = out // LANES
    lane = out % LANES
    eighth = lane % (2 * MARGIN)
    source = side_source(lane, column, cols)
    to_up = (column == plan.patches) & (eighth < MARGIN)
    to_down = (column == plan.patches + 1) & (eighth >= MARGIN)
    source = jnp.where(column < plan.patches, source, -1)
    source = jnp.where(to_up, cols - MARGIN + eighth, source)
    source = jnp.where(to_down, eighth - MARGIN, source)
    hit = jnp.where(col == source, 1.0, 0.0)
    which = iota((1, n_side), 1) % LANES // (2 * MARGIN)
    for s in range(plan.states):
        for t in range(DEPTH):
            at = s * DEPTH + t
            side_ref[at * cols : (at + 1) * cols, :] = jnp.where(which == at, hit, 0.0).astype(bf16)
    lhs = [
        jnp.concatenate(
            [
                jnp.concatenate([turned[s, b * DEPTH + t] for b in range(plan.bands)], axis=0)
                for t in range(DEPTH)
            ],
            axis=1,
        )
        for s in range(plan.states)
    ]
    zero = jnp.zeros((plan.members, LANES), bf16)

    def put(band, inner, column, value):
        for g, position in plan.band_slots(band):
            buf_ref[plan.index_of[(g, column)], position * plan.per_band + inner] = value

    m = plan.members
    for s in range(plan.states):
        center = dot(lhs[s], q_ref[...]).astype(bf16)
        for b in range(plan.bands):
            for c in range(plan.patches):
                put(b, s, c, center[b * m : (b + 1) * m, c * LANES : (c + 1) * LANES])
    sides = dot(jnp.concatenate(lhs, axis=1), side_ref[...]).astype(bf16)
    for b in range(plan.bands):
        for c in range(plan.patches):
            put(b, plan.states, c, sides[b * m : (b + 1) * m, c * LANES : (c + 1) * LANES])
    at = plan.patches * LANES
    up_ref[...] = sides[:, at : at + LANES]
    down_ref[...] = sides[:, at + LANES : at + 2 * LANES]
    if plan.full:
        for c in range(plan.patches):
            for inner in range(plan.per_band):
                buf_ref[plan.index_of[(0, c)], inner] = zero
                last = (plan.slot_bands - 1) * plan.per_band + inner
                buf_ref[plan.index_of[(plan.groups - 1, c)], last] = zero


def split2(a):
    high = a.astype(bf16)
    return high, (a - high.astype(f32)).astype(bf16)


def window_place(entry):
    height = DEPTH + 2 * MARGIN
    width = SPAN + 2 * MARGIN
    plane = height * width
    state = sum((entry >= plane * n).astype(i32) for n in range(1, 4))
    rest = entry - state * plane
    row = (rest * 1639) >> 16
    col = rest - row * width
    band = row >> 2
    inner = row & 3
    center = (col >= MARGIN) & (col < MARGIN + SPAN)
    eighth = jnp.where(col < MARGIN, col, col - SPAN)
    lane = jnp.where(center, inner * SPAN + col - MARGIN, state * SPAN + inner * 2 * MARGIN + eighth)
    group = band * 5 + jnp.where(center, state, 4)
    return group, lane


def map_kernel(patches, table, count_ref, factor_ref, cell_ref, class_ref, value_ref, inv_ref, out_ref):
    slots = cell_ref.shape[1]
    group, lane = window_place(cell_ref[...])
    classes = class_ref[...]
    factor = jnp.zeros(classes.shape, f32)
    for n in range(table):
        factor = jnp.where(classes == n, factor_ref[n], factor)
    weight = inv_ref[...] * factor
    order = iota((1, slots), 1)
    for p in range(patches):
        live = jnp.where(order < count_ref[0, p], weight[p : p + 1], 0.0)
        hot = one_hot(iota((LANES, slots), 0) == lane[p : p + 1])
        pick = iota((MAP_ROWS, slots), 0) == group[p : p + 1]
        parts = []
        for source in (live, live * value_ref[p : p + 1]):
            for _ in range(3):
                high = source.astype(bf16).astype(f32)
                parts.append(jnp.where(pick, high, 0.0).astype(bf16))
                source = source - high
        maps = lax.dot_general(
            jnp.concatenate(parts, axis=0), hot, (((1,), (1,)), ((), ())), preferred_element_type=f32
        )
        n = MAP_ROWS
        w_high, w_low = split2(maps[:n] + maps[n : 2 * n] + maps[2 * n : 3 * n])
        v_high, v_low = split2(maps[3 * n : 4 * n] + maps[4 * n : 5 * n] + maps[5 * n :])
        out_ref[p] = jnp.concatenate([w_high, w_low, v_high, v_low], axis=0)


def join_kernel(plan, own_ref, buf_in, maps_ref, left_ref, right_ref, buf_ref):
    m = plan.members
    buf_ref[:, : plan.field] = buf_in[:, : plan.field]
    for b in range(plan.bands):
        for column, strip in ((0, left_ref), (plan.patches - 1, right_ref)):
            extra = strip[b * m : (b + 1) * m]
            for g, position in plan.band_slots(b):
                at = (plan.index_of[(g, column)], position * plan.per_band + plan.states)
                buf_ref[at] = buf_in[at] + extra
    for i, (g, c) in enumerate(plan.place):
        piece = jnp.where(own_ref[0] == g, maps_ref[c], jnp.zeros_like(maps_ref[c]))
        for n in range(plan.map_groups):
            buf_ref[i, plan.field + n] = piece[n * m : (n + 1) * m]


def mm3(ah, al, bh, bl):
    return dot(jnp.concatenate([ah, ah, al], axis=1), jnp.concatenate([bh, bl, bh], axis=0))


def analyse_kernel(plan, map_at, place_ref, x_ref, maps_ref, out_ref, xs, avgs, scaled, lead):
    total = plan.total
    sources, _, piece_rows, _ = x_ref.shape
    per_band, states, patches = plan.per_band, plan.states, plan.patches
    window = 3 * per_band * LANES
    group = place_ref[0]
    shift = place_ref[1]
    if not plan.full:
        blank = jnp.zeros((total, per_band * LANES), bf16)
        if plan.slot_bands == patches:
            edges = (0, patches + 1)
            for edge in edges:
                xs[:, edge * per_band * LANES : (edge + 1) * per_band * LANES] = blank
                avgs[edge * 8 : edge * 8 + 8] = jnp.zeros((8, LANES), f32)
        else:
            edge = jnp.where(shift == 1, 0, patches + 1)
            xs[:, pl.ds(pl.multiple_of(edge * per_band * LANES, LANES), per_band * LANES)] = blank
            avgs[pl.ds(pl.multiple_of(edge * 8, 8), 8)] = jnp.zeros((8, LANES), f32)
    for b in range(plan.slot_bands):
        means = []
        for inner in range(per_band):
            at = b * per_band + inner
            raw = jnp.concatenate([x_ref[n, at] for n in range(sources)], axis=0).astype(f32)
            mean = jnp.sum(raw, axis=0, keepdims=True) / total
            means.append(mean)
            lanes = pl.multiple_of((shift * per_band + at) * LANES, LANES)
            xs[:, pl.ds(lanes, LANES)] = (raw - mean).astype(bf16)
        means.append(jnp.zeros((8 - per_band, LANES), f32))
        avgs[pl.ds(pl.multiple_of((b + shift) * 8, 8), 8)] = jnp.concatenate(means, axis=0)
    eye = jnp.where(iota((total, total), 0) == iota((total, total), 1), 1.0, 0.0)
    grams, forcings, norms = [], [], []
    for q in range(patches):
        n_map = maps_ref.shape[1] - map_at
        maps = jnp.concatenate(
            [maps_ref[patches * group + q, map_at + n] for n in range(n_map)], axis=0
        ).astype(f32)
        n = MAP_ROWS
        weight = maps[:n] + maps[n : 2 * n]
        value = maps[2 * n : 3 * n] + maps[3 * n :]
        lead[...] = jnp.zeros_like(lead)
        for d in range(3):
            for inner in range(per_band):
                at = d * per_band + inner
                lanes = (q * per_band + at) * LANES
                w = weight[at : at + 1]
                here = slice(at * LANES, (at + 1) * LANES)
                scaled[q, :total, here] = (xs[:, lanes : lanes + LANES].astype(f32) * w).astype(bf16)
                row = (q + d) * 8 + inner
                v = value[at : at + 1] - w * avgs[row : row + 1]
                for part in range(3):
                    high = v.astype(bf16).astype(f32)
                    lead[part : part + 1, here] = high
                    v = v - high
        scaled[q, total:] = lead[...].astype(bf16)
        first = q * per_band * LANES
        both = lax.dot_general(
            scaled[q],
            xs[:, first : first + window],
            (((1,), (1,)), ((), ())),
            preferred_element_type=f32,
        )
        gram = both[:total] + ((total - 1) / INFLATION) * eye
        forcings.append(both[total : total + 1] + both[total + 1 : total + 2] + both[total + 2 : total + 3])
        norm = jnp.sqrt(jnp.sum(jnp.sum(gram * gram, axis=1, keepdims=True), axis=0, keepdims=True))
        norms.append(norm)
        grams.append(gram / norm)
    factors, iterates, roots = [], [], []
    for q in range(patches):
        y = split2(grams[q])
        f = split2(1.5 * eye - 0.5 * grams[q])
        iterates.append(split2(mm3(*y, *f)))
        roots.append(f)
    for sweep in range(1, ITERS):
        for q in range(patches):
            f = split2(1.5 * eye - 0.5 * mm3(*roots[q], *iterates[q]))
            if sweep + 1 < ITERS:
                iterates[q] = split2(mm3(*iterates[q], *f))
                roots[q] = split2(mm3(*roots[q], *f))
            else:
                roots[q] = mm3(*roots[q], *f)
    for q in range(patches):
        root = roots[q]
        force = jnp.broadcast_to(forcings[q], (8, total))
        part = jnp.dot(force, root, precision=lax.Precision.HIGHEST, preferred_element_type=f32)
        move = jnp.dot(part, root, precision=lax.Precision.HIGHEST, preferred_element_type=f32)
        move = move[:1] / norms[q]
        transform = (jnp.sqrt((total - 1.0) / norms[q]) * root + move).astype(bf16)
        first = (q + 1) * per_band * LANES
        analysed = dot(transform, xs[:, first : first + states * LANES])
        for s in range(states):
            row = (q + 1) * 8 + s
            value = (analysed[:, s * LANES : (s + 1) * LANES] + avgs[row : row + 1]).astype(bf16)
            for n in range(sources):
                out_ref[n, q * states + s] = value[n * piece_rows : (n + 1) * piece_rows]


def unpack_kernel(plan, in_ref, out_ref, q_ref, turned):
    half = 16
    m, rows, cols, states = plan.members, plan.rows, plan.cols, plan.states
    wide = DEPTH * cols
    r = iota((wide, wide), 0)
    k = iota((wide, wide), 1)
    q_ref[...] = one_hot(
        (k // cols == (r % LANES) // SPAN) & (k % cols == (r // LANES) * SPAN + r % SPAN)
    )
    for s in range(states):
        lhs = []
        for b in range(plan.bands):
            g, q = b // plan.patches, b % plan.patches
            lhs.append(
                jnp.concatenate(
                    [in_ref[plan.index_of[(g, c)], q * states + s] for c in range(plan.patches)], axis=1
                )
            )
        opened = dot(jnp.concatenate(lhs, axis=0), q_ref[...]).astype(bf16)
        for b in range(plan.bands):
            for t in range(DEPTH):
                turned[s, b * DEPTH + t] = opened[b * m : (b + 1) * m, t * cols : (t + 1) * cols]
    span = half * rows
    r = iota((span, span), 0)
    k = iota((span, span), 1)
    perm = one_hot((k % half == r // rows) & (k // half == r % rows))
    for s in range(states):
        for h in range(m // half):
            piece = turned[s, :, h * half : (h + 1) * half, :].reshape(span, cols)
            out_ref[h * half : (h + 1) * half, s] = (
                dot(perm, piece).astype(bf16).reshape(half, rows, cols)
            )


def shifts(axis):
    count = lax.axis_size(axis)
    forward = [(i, i + 1) for i in range(count - 1)]
    return forward, [(b, a) for a, b in forward]


def pack_plain(plan, x):
    m, s, b = plan.members, plan.states, plan.bands
    bands = x.reshape(m, s, b, DEPTH, plan.cols)
    center = bands.reshape(m, s, b, DEPTH, plan.patches, SPAN).transpose(4, 2, 1, 0, 3, 5)
    center = center.reshape(plan.patches, b, s, m, LANES)
    padded = jnp.pad(bands, ((0, 0),) * 4 + ((MARGIN, MARGIN),))
    sides = jnp.stack(
        [
            jnp.concatenate(
                [
                    padded[..., c * SPAN : c * SPAN + MARGIN],
                    padded[..., (c + 1) * SPAN + MARGIN : (c + 1) * SPAN + 2 * MARGIN],
                ],
                axis=-1,
            )
            for c in range(plan.patches)
        ]
    )
    sides = sides.transpose(0, 3, 1, 2, 4, 5).reshape(plan.patches, b, 1, m, LANES)
    whole = jnp.concatenate([center, sides], axis=2)
    whole = jnp.pad(whole, ((0, 0), (1, 1)) + ((0, 0),) * 3)
    slots = []
    for g, c in plan.place:
        first = plan.first_band(g) + 1
        piece = whole[c, first : first + plan.slot_bands].reshape(plan.field, m, LANES)
        slots.append(jnp.pad(piece, ((0, plan.map_groups), (0, 0), (0, 0))))
    empty = jnp.zeros_like(bands[..., :MARGIN])
    strips = []
    for pair in ((bands[..., -MARGIN:], empty), (empty, bands[..., :MARGIN])):
        strip = jnp.concatenate(pair, axis=-1).transpose(2, 0, 1, 3, 4)
        strips.append(strip.reshape(b * m, LANES))
    return jnp.stack(slots), strips[0], strips[1]


def unpack_plain(plan, arrived):
    m, s, b = plan.members, plan.states, plan.bands
    bands = []
    for band in range(b):
        g, q = band // plan.patches, band % plan.patches
        pieces = jnp.stack(
            [arrived[plan.index_of[(g, c)], q * s : (q + 1) * s] for c in range(plan.patches)]
        )
        pieces = pieces.reshape(plan.patches, s, m, DEPTH, SPAN).transpose(2, 1, 3, 0, 4)
        bands.append(pieces.reshape(m, s, DEPTH, plan.cols))
    return jnp.concatenate(bands, axis=2)


def local(x, tally, cells, classes, readings, inverse, factors):
    count = lax.axis_size("mem")
    plan = Plan(x.shape, count, x.shape[1])
    patches = plan.patches
    index = lax.axis_index("mem")
    aligned = plan.members % 16 == 0
    buffer = (count, plan.slot, plan.members, LANES)
    strip = (plan.bands * plan.members, LANES)
    if aligned:
        packed, upward, downward = pl.pallas_call(
            functools.partial(pack_kernel, plan),
            out_shape=(
                jax.ShapeDtypeStruct(buffer, bf16),
                jax.ShapeDtypeStruct(strip, bf16),
                jax.ShapeDtypeStruct(strip, bf16),
            ),
            in_specs=[VMEM],
            out_specs=(VMEM, VMEM, VMEM),
            scratch_shapes=[
                pltpu.VMEM((plan.states, plan.rows, plan.members, plan.cols), bf16),
                pltpu.VMEM((DEPTH * plan.cols, DEPTH * plan.cols), bf16),
                pltpu.VMEM((plan.states * DEPTH * plan.cols, (patches + 2) * LANES), bf16),
            ],
            compiler_params=PARAMS,
            name="pack",
        )(x)
    else:
        packed, upward, downward = pack_plain(plan, x)
    forward, backward = shifts("col")
    left = lax.ppermute(upward, "col", forward)
    right = lax.ppermute(downward, "col", backward)
    slots = cells.shape[-1]
    maps = pl.pallas_call(
        functools.partial(map_kernel, patches, factors.shape[0]),
        out_shape=jax.ShapeDtypeStruct((patches, 4 * MAP_ROWS, LANES), bf16),
        in_specs=[SMEM, SMEM, VMEM, VMEM, VMEM, VMEM],
        out_specs=VMEM,
        compiler_params=PARAMS,
        name="maps",
    )(
        tally,
        factors,
        cells.reshape(patches, slots),
        classes.reshape(patches, slots),
        readings.reshape(patches, slots),
        inverse.reshape(patches, slots),
    )
    if aligned:
        packed = pl.pallas_call(
            functools.partial(join_kernel, plan),
            out_shape=jax.ShapeDtypeStruct(buffer, bf16),
            in_specs=[SMEM, VMEM, VMEM, VMEM, VMEM],
            out_specs=VMEM,
            compiler_params=PARAMS,
            name="join",
        )((index // patches).reshape(1), packed, maps, left, right)
    else:
        for b in range(plan.bands):
            at = slice(b * plan.members, (b + 1) * plan.members)
            for column, extra in ((0, left[at]), (patches - 1, right[at])):
                for g, position in plan.band_slots(b):
                    here = position * plan.per_band + plan.states
                    packed = packed.at[plan.index_of[(g, column)], here].add(extra)
        for i, (g, c) in enumerate(plan.place):
            piece = jnp.where(index // patches == g, maps[c], 0).reshape(-1, plan.members, LANES)
            packed = packed.at[i, plan.field :].set(piece)
    arrived = lax.all_to_all(packed, "mem", split_axis=0, concat_axis=0, tiled=True)
    group = jnp.asarray([g for g, _ in plan.place], i32)[index]
    shift = jnp.where(group == 0, 0 if plan.full else 1, 0)
    where = jnp.stack([group, shift]).astype(i32)
    if aligned:
        fields, map_source, map_at = arrived, arrived, plan.field
        pieces = (count, plan.members)
    else:
        fields = arrived[:, : plan.field].transpose(1, 0, 2, 3).reshape(1, plan.field, plan.total, LANES)
        map_source = arrived[:, plan.field :].reshape(count, 1, 4 * MAP_ROWS, LANES)
        map_at = 0
        pieces = (1, plan.total)
    bands = (patches + 2) * plan.per_band
    analysed = pl.pallas_call(
        functools.partial(analyse_kernel, plan, map_at),
        out_shape=jax.ShapeDtypeStruct((pieces[0], patches * plan.states, pieces[1], LANES), bf16),
        in_specs=[SMEM, VMEM, VMEM],
        out_specs=VMEM,
        scratch_shapes=[
            pltpu.VMEM((plan.total, bands * LANES), bf16),
            pltpu.VMEM(((patches + 2) * 8, LANES), f32),
            pltpu.VMEM((patches, plan.total + 16, 3 * plan.per_band * LANES), bf16),
            pltpu.VMEM((16, 3 * plan.per_band * LANES), f32),
        ],
        compiler_params=PARAMS,
        name="analyse",
    )(where, fields, map_source)
    if not aligned:
        analysed = analysed.reshape(-1, count, plan.members, LANES).transpose(1, 0, 2, 3)
    returned = lax.all_to_all(analysed, "mem", split_axis=0, concat_axis=0, tiled=True)
    if not aligned:
        return unpack_plain(plan, returned)
    return pl.pallas_call(
        functools.partial(unpack_kernel, plan),
        out_shape=jax.ShapeDtypeStruct(x.shape, bf16),
        in_specs=[VMEM],
        out_specs=VMEM,
        scratch_shapes=[
            pltpu.VMEM((DEPTH * plan.cols, DEPTH * plan.cols), bf16),
            pltpu.VMEM((plan.states, plan.rows, plan.members, plan.cols), bf16),
        ],
        compiler_params=PARAMS,
        name="unpack",
    )(returned)


def solution(mesh):
    placed = (
        P("mem", None, None, "col"),
        P("mem", "col"),
        P("mem", "col", None),
        P("mem", "col", None),
        P("mem", "col", None),
        P("mem", "col", None),
        P(),
    )
    return jax.shard_map(
        local, mesh=mesh, in_specs=placed, out_specs=P("mem", None, None, "col"), check_vma=False
    )
```

time: 391 us -> 76.9 us (0.20)
  blocking collectives: 174 us -> 17.8 us
  local copies, waits for them, and re-layouts: 145 us -> 6.15 us
  matrix products: 28.2 us -> 0 us
  other arithmetic: 27.2 us -> 0.72 us
  Pallas kernels: 0 us -> 19.7 us
  waiting for transfers between devices: 3.97 us -> 21.1 us
    all_to_all x2 -> x1, blocking collectives: 174 us -> 17.8 us  [local(): lax.all_to_all(analysed, 'mem', split_axis=0, concat_axis=0, tiled=True)]
    gather x24 -> x0, local copies, waits for them, and re-layouts: 93 us -> none  [the longest x16 54.3 us: observe(): observed = jnp.take_along_axis(anomaly_flat, cell_ids[:, None, :], axis=2)]
    slice x12 -> x0, local copies, waits for them, and re-layouts: 31.5 us -> none  [the longest x5 19.8 us: local(): deviation_matrix[:, :, :, sector_index * SECTOR_SPAN:sector_index * SECTO...]
    dot_general x31 -> x0, matrix products: 28.2 us -> none  [the longest x1 7.08 us: local(): lax.dot_general(unit_weights, enlarged_piece, (((0,), (0,)), ((), ())), p...]
    all_to_all x0 -> x1, waiting for transfers between devices: none -> 21.1 us  [local(): lax.all_to_all(packed, 'mem', split_axis=0, concat_axis=0, tiled=True)]
    pallas_call x0 -> x5, Pallas kernels: none -> 19.7 us  [the longest x1 11.1 us: local(): pl.pallas_call(functools.partial(analyse_kernel, plan, map_at), out_shape...]
    convert_element_type x2 -> x0, other arithmetic: 8.78 us -> none  [the longest x1 8.04 us: local(): (enlarged_piece.astype(jnp.float32) - predicted_average).astype(jnp.bfloa...]
    sub x8 -> x0, other arithmetic: 6.27 us -> none  [observe(): innovation = values - jnp.take_along_axis(average_flat, cell_ids, axis=1)]
  transfers between devices with their start and end apart: 4 -> 3, of which waited for: 2 -> 1; matrix products, arithmetic and copies ran while one was open for 2% -> 2% of each run, Pallas kernels for 0% -> 2%
where the time goes in v1:
time: 76.9 us; the launch traced here: 76.3 us
  waiting for transfers between devices  21.1 us (27%)
  Pallas kernels  19.7 us (26%)
  blocking collectives  17.8 us (23%)
  starting transfers between devices  10.1 us (13%)
  local copies, waits for them, and re-layouts  6.15 us (8%)
    all_to_all x1, waiting for transfers between devices, local(): lax.all_to_all(packed, 'mem', split_axis=0, concat_axis=0, tiled=True)  21.1 us
    all_to_all x1, blocking collectives, local(): lax.all_to_all(analysed, 'mem', split_axis=0, concat_axis=0, tiled=True)  17.8 us
    pallas_call x1, Pallas kernels, local(): pl.pallas_call(functools.partial(analyse_kernel, plan, map_at), out_shape...  11.1 us
    unnamed x16, local copies, waits for them, and re-layouts  5.56 us
    ppermute x1, starting transfers between devices, local(): left = lax.ppermute(upward, 'col', forward)  4.96 us
    all_to_all x1, starting transfers between devices, local(): lax.all_to_all(packed, 'mem', split_axis=0, concat_axis=0, tiled=True)  3.85 us
    pallas_call x1, Pallas kernels, local(): pl.pallas_call(functools.partial(pack_kernel, plan), out_shape=(jax.Shape...  2.86 us
    pallas_call x1, Pallas kernels, local(): pl.pallas_call(functools.partial(unpack_kernel, plan), out_shape=jax.Shap...  2.84 us
  transfers between devices with their start and end apart: 3, of which 1 were waited for; matrix products, arithmetic and copies ran while one was open for 2% of the time, Pallas kernels for 2%

profile of v1, /device:TPU:0, one launch (start us, length us, event | category | flops | bytes accessed | tf_op | source)
XLA Modules:
  0.0 76.3 jit_solution(6171340145603985737)
XLA Ops:
  0.0 0.0 copy-start
  0.0 1.2 %copy-done = bf16[32,4,32,128]{3,2,1,0:T(8,128)(2,1)S(1)} copy-done((bf16[32,4,32,128]{3,2,1,0:T(8,128)(2,1)S(1)}, bf16[32,4,32,128]{3,2,1,0:T(8,128)(2,1)}, u32[]{:S(2)}) %copy-start) | copy-done | bytes 1048600
  1.2 2.9 %pack.1 = (bf16[8,27,32,128]{3,2,1,0:T(8,128)(2,1)S(1)}, bf16[256,128]{1,0:T(8,128)(2,1)S(1)}, bf16[256,128]{1,0:T(8,128)(2,1)S(1)}) custom-call(bf16[32,4,32,128]{3,2,1,0:T(8,128)(2,1)S(1)} %copy-done), custom_call_target="tpu_custom_call" | custom-call | tf_op jit(solution)/shard_map/pack/pallas_call | solution.py:414
  4.1 5.0 %collective-permute-start = (bf16[256,128]{1,0:T(8,128)(2,1)S(1)}, bf16[256,128]{1,0:T(8,128)(2,1)S(1)}, u32[]{:S(2)}, u32[]{:S(2)}) collective-permute-start(bf16[256,128]{1,0:T(8,128)(2,1)S(1)} %get-tuple-element.9), channel_id=1, source_target_pairs={{0,1},{1,2},{2,3},{4,5},{5,6},{6,7},{8,9},{9,10},{10,11},{12,13},{... | collective-permute-start | bytes 196616 | tf_op jit(solution)/shard_map/ppermute | solution.py:434
  9.1 1.3 %collective-permute-start.1 = (bf16[256,128]{1,0:T(8,128)(2,1)S(1)}, bf16[256,128]{1,0:T(8,128)(2,1)S(1)}, u32[]{:S(2)}, u32[]{:S(2)}) collective-permute-start(bf16[256,128]{1,0:T(8,128)(2,1)S(1)} %get-tuple-element.10), channel_id=1, source_target_pairs={{1,0},{2,1},{3,2},{5,4},{6,5},{7,6},{9,8},{10,9},{11,10},{13,12},{... | collective-permute-start | bytes 196616 | tf_op jit(solution)/shard_map/ppermute | solution.py:435
  10.4 0.0 copy-start.1
  10.4 0.7 copy-done.1
  11.1 0.0 copy-start.2
  11.1 0.8 copy-done.2
  11.9 0.0 copy-start.3
  11.9 0.8 copy-done.3
  12.7 0.0 copy-start.4
  12.7 0.8 copy-done.4
  13.4 0.0 copy-start.5
  13.4 0.7 copy-done.5
  14.1 0.0 copy-start.6
  14.1 0.7 copy-done.6
  14.7 1.5 %maps.1.maps_ref = bf16[4,64,128]{2,1,0:T(8,128)(2,1)S(1)} custom-call(s32[1,4]{1,0:T(1,128)S(1)} %copy-done.5, f32[16]{0:T(128)S(1)} %copy-done.6, s32[4,2048]{1,0:T(4,128)S(1)} %bitcast.5, s32[4,2048]{1,0:T(4,128)S(1)} %bitcast.6, f32[4,2048]{1,0:T(4,128)S(1)} %bitcast.7, f32[4,2048]{1,0:T(4,128)S(1)} %bitcast.8), custom_call_target="tpu_custom_call" | custom-call | tf_op jit(solution)/shard_map/maps/pallas_call | solution.py:437
  16.2 0.0 collective-permute-done.left_ref
  16.2 0.0 collective-permute-done.1.right_ref
  16.2 1.4 %join.1 = bf16[8,27,32,128]{3,2,1,0:T(8,128)(2,1)} custom-call(s32[1]{0:T(128)} %bitcast.own_ref, bf16[8,27,32,128]{3,2,1,0:T(8,128)(2,1)S(1)} %get-tuple-element.8.buf_in, bf16[4,64,128]{2,1,0:T(8,128)(2,1)S(1)} %maps.1.maps_ref, bf16[256,128]{1,0:T(8,128)(2,1)S(1)} %collective-permute-done.left_ref, bf16[256,128]{1,0:T(8,128)(2,1)S(1)} %collective-permute-done.1.right_ref), custom_call_target="tpu_custom_call" | custom-call | tf_op jit(solution)/shard_map/join/pallas_call | solution.py:453
  17.6 0.0 copy-start.7
  17.6 3.9 %all-to-all-start = ((bf16[8,27,32,128]{3,2,1,0:T(8,128)(2,1)}), bf16[8,27,32,128]{3,2,1,0:T(8,128)(2,1)S(1)}, u32[]{:S(2)}, u32[]{:S(2)}) async-start(bf16[8,27,32,128]{3,2,1,0:T(8,128)(2,1)} %join.1), calls=%async_computation | async-start | bytes 3538944 | tf_op jit(solution)/shard_map/all_to_all | solution.py:471
  21.5 0.0 copy-done.7
  21.5 0.6 dynamic_slice.3
  22.7 0.7 pad_add_fusion.place_ref
  23.4 21.1 %all-to-all-done.x_ref.maps_ref = bf16[8,27,32,128]{3,2,1,0:T(8,128)(2,1)S(1)} async-done(((bf16[8,27,32,128]{3,2,1,0:T(8,128)(2,1)}), bf16[8,27,32,128]{3,2,1,0:T(8,128)(2,1)S(1)}, u32[]{:S(2)}, u32[]{:S(2)}) %all-to-all-start) | async-done | bytes 1769504 | tf_op jit(solution)/shard_map/all_to_all | solution.py:471
  44.6 11.1 %analyse.1 = bf16[8,16,32,128]{3,2,1,0:T(8,128)(2,1)S(1)} custom-call(s32[2]{0:T(128)S(1)} %pad_add_fusion.place_ref, bf16[8,27,32,128]{3,2,1,0:T(8,128)(2,1)S(1)} %all-to-all-done.x_ref.maps_ref, bf16[8,27,32,128]{3,2,1,0:T(8,128)(2,1)S(1)} %all-to-all-done.x_ref.maps_ref), custom_call_target="tpu_custom_call" | custom-call | tf_op jit(solution)/shard_map/analyse/pallas_call | solution.py:484
  55.7 17.8 %all_to_all.10.in_ref = bf16[8,16,32,128]{3,2,1,0:T(8,128)(2,1)S(1)} all-to-all(bf16[8,16,32,128]{3,2,1,0:T(8,128)(2,1)S(1)} %analyse.1), channel_id=1, replica_groups=mesh['mem'=8,'col'=4] {'mem'}, dimensions={0} | all-to-all | bytes 2097152 | tf_op jit(solution)/shard_map/all_to_all | solution.py:500
  73.4 2.8 %unpack.1 = bf16[32,4,32,128]{3,2,1,0:T(8,128)(2,1)} custom-call(bf16[8,16,32,128]{3,2,1,0:T(8,128)(2,1)S(1)} %all_to_all.10.in_ref), custom_call_target="tpu_custom_call" | custom-call | tf_op jit(solution)/shard_map/unpack/pallas_call | solution.py:503
Async XLA Ops:
  0.0 1.2 %copy-start = (bf16[32,4,32,128]{3,2,1,0:T(8,128)(2,1)S(1)}, bf16[32,4,32,128]{3,2,1,0:T(8,128)(2,1)}, u32[]{:S(2)}) copy-start(bf16[32,4,32,128]{3,2,1,0:T(8,128)(2,1)} %x_ref.1) | copy-start | bytes 3145732
  4.1 12.1 %collective-permute-start = (bf16[256,128]{1,0:T(8,128)(2,1)S(1)}, bf16[256,128]{1,0:T(8,128)(2,1)S(1)}, u32[]{:S(2)}, u32[]{:S(2)}) collective-permute-start(bf16[256,128]{1,0:T(8,128)(2,1)S(1)} %get-tuple-element.9), channel_id=1, source_target_pairs={{0,1},{1,2},{2,3},{4,5},{5,6},{6,7},{8,9},{9,10},{10,11},{12,13},{... | collective-permute-start | bytes 196616 | tf_op jit(solution)/shard_map/ppermute | solution.py:434
  9.1 7.2 %collective-permute-start.1 = (bf16[256,128]{1,0:T(8,128)(2,1)S(1)}, bf16[256,128]{1,0:T(8,128)(2,1)S(1)}, u32[]{:S(2)}, u32[]{:S(2)}) collective-permute-start(bf16[256,128]{1,0:T(8,128)(2,1)S(1)} %get-tuple-element.10), channel_id=1, source_target_pairs={{1,0},{2,1},{3,2},{5,4},{6,5},{7,6},{9,8},{10,9},{11,10},{13,12},{... | collective-permute-start | bytes 196616 | tf_op jit(solution)/shard_map/ppermute | solution.py:435
  10.4 0.8 copy-start.1
  11.1 0.8 copy-start.2
  11.9 0.8 copy-start.3
  12.7 0.8 copy-start.4
  13.4 0.7 copy-start.5
  14.1 0.7 copy-start.6
  17.6 3.9 %copy-start.7 = (s32[8]{0:T(128)S(1)}, s32[8]{0:T(128)}, u32[]{:S(2)}) copy-start(s32[8]{0:T(128)} %constant.33.clone) | copy-start | bytes 100
  17.6 27.0 %all-to-all-start = ((bf16[8,27,32,128]{3,2,1,0:T(8,128)(2,1)}), bf16[8,27,32,128]{3,2,1,0:T(8,128)(2,1)S(1)}, u32[]{:S(2)}, u32[]{:S(2)}) async-start(bf16[8,27,32,128]{3,2,1,0:T(8,128)(2,1)} %join.1), calls=%async_computation | async-start | bytes 3538944 | tf_op jit(solution)/shard_map/all_to_all | solution.py:471

commit v2 on v1

--- a/solution.py
+++ b/solution.py
@@ -57,6 +57,12 @@
         self.slot = self.field + self.map_groups
         self.index_of = {p: i for i, p in enumerate(self.place)}
 
+    def group_of(self, index):
+        return sum(jnp.where(index == i, g, 0) for i, (g, _) in enumerate(self.place))
+
+    def shift_of(self, group):
+        return jnp.where(group == 0, 0 if self.full else 1, 0)
+
     def first_band(self, group):
         low = self.patches * group - 1
         return low if self.full else max(low, 0)
@@ -76,7 +82,7 @@
     return jnp.where(eighth < MARGIN, low, high)
 
 
-def pack_kernel(plan, x_ref, buf_ref, up_ref, down_ref, turned, q_ref, side_ref):
+def pack_kernel(plan, x_ref, buf_ref, turned, q_ref):
     half = 16
     rows, cols = plan.rows, plan.cols
     span = half * rows
@@ -95,6 +101,35 @@
     q_ref[...] = one_hot(
         (r // cols == (k % LANES) // SPAN) & (r % cols == (k // LANES) * SPAN + k % SPAN)
     )
+    m = plan.members
+    for s in range(plan.states):
+        center = dot(banded(plan, turned, s), q_ref[...]).astype(bf16)
+        for b in range(plan.bands):
+            for c in range(plan.patches):
+                value = center[b * m : (b + 1) * m, c * LANES : (c + 1) * LANES]
+                for g, position in plan.band_slots(b):
+                    buf_ref[plan.index_of[(g, c)], position * plan.states + s] = value
+    if plan.full:
+        zero = jnp.zeros((plan.members, LANES), bf16)
+        for c in range(plan.patches):
+            for s in range(plan.states):
+                buf_ref[plan.index_of[(0, c)], s] = zero
+                last = (plan.slot_bands - 1) * plan.states + s
+                buf_ref[plan.index_of[(plan.groups - 1, c)], last] = zero
+
+
+def banded(plan, turned, s):
+    return jnp.concatenate(
+        [
+            jnp.concatenate([turned[s, b * DEPTH + t] for b in range(plan.bands)], axis=0)
+            for t in range(DEPTH)
+        ],
+        axis=1,
+    )
+
+
+def sides_kernel(plan, turned, own_ref, up_ref, down_ref, side_ref):
+    cols = plan.cols
     n_side = (plan.patches + 2) * LANES
     col = iota((cols, n_side), 0)
     out = iota((cols, n_side), 1)
@@ -113,41 +148,13 @@
         for t in range(DEPTH):
             at = s * DEPTH + t
             side_ref[at * cols : (at + 1) * cols, :] = jnp.where(which == at, hit, 0.0).astype(bf16)
-    lhs = [
-        jnp.concatenate(
-            [
-                jnp.concatenate([turned[s, b * DEPTH + t] for b in range(plan.bands)], axis=0)
-                for t in range(DEPTH)
-            ],
-            axis=1,
-        )
-        for s in range(plan.states)
-    ]
-    zero = jnp.zeros((plan.members, LANES), bf16)
-
-    def put(band, inner, column, value):
-        for g, position in plan.band_slots(band):
-            buf_ref[plan.index_of[(g, column)], position * plan.per_band + inner] = value
-
-    m = plan.members
-    for s in range(plan.states):
-        center = dot(lhs[s], q_ref[...]).astype(bf16)
-        for b in range(plan.bands):
-            for c in range(plan.patches):
-                put(b, s, c, center[b * m : (b + 1) * m, c * LANES : (c + 1) * LANES])
-    sides = dot(jnp.concatenate(lhs, axis=1), side_ref[...]).astype(bf16)
-    for b in range(plan.bands):
-        for c in range(plan.patches):
-            put(b, plan.states, c, sides[b * m : (b + 1) * m, c * LANES : (c + 1) * LANES])
+    lhs = jnp.concatenate([banded(plan, turned, s) for s in range(plan.states)], axis=1)
+    sides = dot(lhs, side_ref[...]).astype(bf16)
+    for c in range(plan.patches):
+        own_ref[c] = sides[:, c * LANES : (c + 1) * LANES]
     at = plan.patches * LANES
     up_ref[...] = sides[:, at : at + LANES]
     down_ref[...] = sides[:, at + LANES : at + 2 * LANES]
-    if plan.full:
-        for c in range(plan.patches):
-            for inner in range(plan.per_band):
-                buf_ref[plan.index_of[(0, c)], inner] = zero
-                last = (plan.slot_bands - 1) * plan.per_band + inner
-                buf_ref[plan.index_of[(plan.groups - 1, c)], last] = zero
 
 
 def split2(a):
@@ -168,7 +175,7 @@
     center = (col >= MARGIN) & (col < MARGIN + SPAN)
     eighth = jnp.where(col < MARGIN, col, col - SPAN)
     lane = jnp.where(center, inner * SPAN + col - MARGIN, state * SPAN + inner * 2 * MARGIN + eighth)
-    group = band * 5 + jnp.where(center, state, 4)
+    group = jnp.where(center, band * 4 + state, 12 + band)
     return group, lane
 
 
@@ -200,54 +207,85 @@
         out_ref[p] = jnp.concatenate([w_high, w_low, v_high, v_low], axis=0)
 
 
-def join_kernel(plan, own_ref, buf_in, maps_ref, left_ref, right_ref, buf_ref):
+def join_kernel(plan, place_ref, own_ref, maps_ref, left_ref, right_ref, *outs):
+    buf_ref = outs[-1]
+    index = place_ref[0]
     m = plan.members
-    buf_ref[:, : plan.field] = buf_in[:, : plan.field]
+    zero = jnp.zeros((m, LANES), bf16)
     for b in range(plan.bands):
-        for column, strip in ((0, left_ref), (plan.patches - 1, right_ref)):
-            extra = strip[b * m : (b + 1) * m]
+        at = slice(b * m, (b + 1) * m)
+        for c in range(plan.patches):
+            value = own_ref[c, at]
+            if c == 0:
+                value = value + left_ref[at]
+            if c == plan.patches - 1:
+                value = value + right_ref[at]
             for g, position in plan.band_slots(b):
-                at = (plan.index_of[(g, column)], position * plan.per_band + plan.states)
-                buf_ref[at] = buf_in[at] + extra
+                buf_ref[plan.index_of[(g, c)], position] = value
+    if plan.full:
+        for c in range(plan.patches):
+            buf_ref[plan.index_of[(0, c)], 0] = zero
+            buf_ref[plan.index_of[(plan.groups - 1, c)], plan.slot_bands - 1] = zero
     for i, (g, c) in enumerate(plan.place):
-        piece = jnp.where(own_ref[0] == g, maps_ref[c], jnp.zeros_like(maps_ref[c]))
+        piece = jnp.where(index // plan.patches == g, maps_ref[c], jnp.zeros_like(maps_ref[c]))
         for n in range(plan.map_groups):
-            buf_ref[i, plan.field + n] = piece[n * m : (n + 1) * m]
+            buf_ref[i, plan.slot_bands + n] = piece[n * m : (n + 1) * m]
+    for k in range(plan.count):
+        outs[k][...] = buf_ref[index ^ k]
 
 
 def mm3(ah, al, bh, bl):
     return dot(jnp.concatenate([ah, ah, al], axis=1), jnp.concatenate([bh, bl, bh], axis=0))
 
 
-def analyse_kernel(plan, map_at, place_ref, x_ref, maps_ref, out_ref, xs, avgs, scaled, lead):
-    total = plan.total
-    sources, _, piece_rows, _ = x_ref.shape
-    per_band, states, patches = plan.per_band, plan.states, plan.patches
-    window = 3 * per_band * LANES
-    group = place_ref[0]
-    shift = place_ref[1]
+def center_of(plan, shift, fields, bands_at, width, xs, avgs):
+    sources = fields.shape[0]
+    total, patches = plan.total, plan.patches
+    step = 8 if width > 1 else 1
     if not plan.full:
-        blank = jnp.zeros((total, per_band * LANES), bf16)
-        if plan.slot_bands == patches:
-            edges = (0, patches + 1)
-            for edge in edges:
-                xs[:, edge * per_band * LANES : (edge + 1) * per_band * LANES] = blank
-                avgs[edge * 8 : edge * 8 + 8] = jnp.zeros((8, LANES), f32)
-        else:
-            edge = jnp.where(shift == 1, 0, patches + 1)
-            xs[:, pl.ds(pl.multiple_of(edge * per_band * LANES, LANES), per_band * LANES)] = blank
-            avgs[pl.ds(pl.multiple_of(edge * 8, 8), 8)] = jnp.zeros((8, LANES), f32)
+        edges = (0, patches + 1)
+        if plan.slot_bands > patches:
+            edges = (jnp.where(shift == 1, 0, patches + 1),)
+        for edge in edges:
+            lanes = pl.ds(edge * width * LANES, width * LANES)
+            if not isinstance(edge, int):
+                lanes = pl.ds(pl.multiple_of(edge * width * LANES, LANES), width * LANES)
+            xs[:, lanes] = jnp.zeros((total, width * LANES), bf16)
+            avgs[pl.ds(edge * step, step)] = jnp.zeros((step, LANES), f32)
     for b in range(plan.slot_bands):
         means = []
-        for inner in range(per_band):
-            at = b * per_band + inner
-            raw = jnp.concatenate([x_ref[n, at] for n in range(sources)], axis=0).astype(f32)
+        for inner in range(width):
+            at = bands_at + b * width + inner
+            raw = jnp.concatenate([fields[n, at] for n in range(sources)], axis=0).astype(f32)
             mean = jnp.sum(raw, axis=0, keepdims=True) / total
             means.append(mean)
-            lanes = pl.multiple_of((shift * per_band + at) * LANES, LANES)
+            lanes = pl.multiple_of(((shift + b) * width + inner) * LANES, LANES)
             xs[:, pl.ds(lanes, LANES)] = (raw - mean).astype(bf16)
-        means.append(jnp.zeros((8 - per_band, LANES), f32))
-        avgs[pl.ds(pl.multiple_of((b + shift) * 8, 8), 8)] = jnp.concatenate(means, axis=0)
+        if width > 1:
+            means.append(jnp.zeros((step - width, LANES), f32))
+        avgs[pl.ds((b + shift) * step, step)] = jnp.concatenate(means, axis=0)
+
+
+def center_kernel(plan, place_ref, x_ref, xs, avgs):
+    shift = plan.shift_of(plan.group_of(place_ref[0]))
+    center_of(plan, shift, x_ref, 0, plan.states, xs, avgs)
+
+
+def analyse_kernel(
+    plan, relative, place_ref, xs, avgs, *rest
+):
+    *pieces, out_ref, side_xs, side_avgs, scaled, lead, gathered = rest
+
+    total, states, patches = plan.total, plan.states, plan.patches
+    sources, _, piece_rows, _ = out_ref.shape
+    group = plan.group_of(place_ref[0])
+    if relative:
+        for k in range(plan.count):
+            gathered[place_ref[0] ^ k] = pieces[k][...]
+        side_ref, maps_ref, map_at = gathered, gathered, plan.slot_bands
+    else:
+        (side_ref, maps_ref), map_at = pieces, 0
+    center_of(plan, plan.shift_of(group), side_ref, 0, 1, side_xs, side_avgs)
     eye = jnp.where(iota((total, total), 0) == iota((total, total), 1), 1.0, 0.0)
     grams, forcings, norms = [], [], []
     for q in range(patches):
@@ -259,26 +297,35 @@
         weight = maps[:n] + maps[n : 2 * n]
         value = maps[2 * n : 3 * n] + maps[3 * n :]
         lead[...] = jnp.zeros_like(lead)
-        for d in range(3):
-            for inner in range(per_band):
-                at = d * per_band + inner
-                lanes = (q * per_band + at) * LANES
-                w = weight[at : at + 1]
-                here = slice(at * LANES, (at + 1) * LANES)
-                scaled[q, :total, here] = (xs[:, lanes : lanes + LANES].astype(f32) * w).astype(bf16)
-                row = (q + d) * 8 + inner
-                v = value[at : at + 1] - w * avgs[row : row + 1]
-                for part in range(3):
-                    high = v.astype(bf16).astype(f32)
-                    lead[part : part + 1, here] = high
-                    v = v - high
+        for at in range(3 * (states + 1)):
+            if at < 3 * states:
+                lanes = (q * states + at) * LANES
+                source = xs[:, lanes : lanes + LANES]
+                row = (q + at // states) * 8 + at % states
+                mean = avgs[row : row + 1]
+            else:
+                row = q + at - 3 * states
+                source = side_xs[:, row * LANES : (row + 1) * LANES]
+                mean = side_avgs[row : row + 1]
+            w = weight[at : at + 1]
+            here = slice(at * LANES, (at + 1) * LANES)
+            scaled[q, :total, here] = (source.astype(f32) * w).astype(bf16)
+            v = value[at : at + 1] - w * mean
+            for part in range(3):
+                high = v.astype(bf16).astype(f32)
+                lead[part : part + 1, here] = high
+                v = v - high
         scaled[q, total:] = lead[...].astype(bf16)
-        first = q * per_band * LANES
+        first = q * states * LANES
+        window = jnp.concatenate(
+            [
+                xs[:, first : first + 3 * states * LANES],
+                side_xs[:, q * LANES : (q + 3) * LANES],
+            ],
+            axis=1,
+        )
         both = lax.dot_general(
-            scaled[q],
-            xs[:, first : first + window],
-            (((1,), (1,)), ((), ())),
-            preferred_element_type=f32,
+            scaled[q], window, (((1,), (1,)), ((), ())), preferred_element_type=f32
         )
         gram = both[:total] + ((total - 1) / INFLATION) * eye
         forcings.append(both[total : total + 1] + both[total + 1 : total + 2] + both[total + 2 : total + 3])
@@ -306,7 +353,7 @@
         move = jnp.dot(part, root, precision=lax.Precision.HIGHEST, preferred_element_type=f32)
         move = move[:1] / norms[q]
         transform = (jnp.sqrt((total - 1.0) / norms[q]) * root + move).astype(bf16)
-        first = (q + 1) * per_band * LANES
+        first = (q + 1) * states * LANES
         analysed = dot(transform, xs[:, first : first + states * LANES])
         for s in range(states):
             row = (q + 1) * 8 + s
@@ -374,19 +421,18 @@
         ]
     )
     sides = sides.transpose(0, 3, 1, 2, 4, 5).reshape(plan.patches, b, 1, m, LANES)
-    whole = jnp.concatenate([center, sides], axis=2)
-    whole = jnp.pad(whole, ((0, 0), (1, 1)) + ((0, 0),) * 3)
-    slots = []
+    center, sides = (jnp.pad(a, ((0, 0), (1, 1)) + ((0, 0),) * 3) for a in (center, sides))
+    slots, side_slots = [], []
     for g, c in plan.place:
-        first = plan.first_band(g) + 1
-        piece = whole[c, first : first + plan.slot_bands].reshape(plan.field, m, LANES)
-        slots.append(jnp.pad(piece, ((0, plan.map_groups), (0, 0), (0, 0))))
+        at = slice(plan.first_band(g) + 1, plan.first_band(g) + 1 + plan.slot_bands)
+        slots.append(center[c, at].reshape(-1, m, LANES))
+        side_slots.append(jnp.pad(sides[c, at, 0], ((0, plan.map_groups), (0, 0), (0, 0))))
     empty = jnp.zeros_like(bands[..., :MARGIN])
     strips = []
     for pair in ((bands[..., -MARGIN:], empty), (empty, bands[..., :MARGIN])):
         strip = jnp.concatenate(pair, axis=-1).transpose(2, 0, 1, 3, 4)
         strips.append(strip.reshape(b * m, LANES))
-    return jnp.stack(slots), strips[0], strips[1]
+    return jnp.stack(slots), jnp.stack(side_slots), strips[0], strips[1]
 
 
 def unpack_plain(plan, arrived):
@@ -407,29 +453,44 @@
     plan = Plan(x.shape, count, x.shape[1])
     patches = plan.patches
     index = lax.axis_index("mem")
+    where = index.reshape(1)
     aligned = plan.members % 16 == 0
-    buffer = (count, plan.slot, plan.members, LANES)
-    strip = (plan.bands * plan.members, LANES)
+    states, members, total = plan.states, plan.members, plan.total
+    strip = (plan.bands * members, LANES)
+    side_slot = (count, plan.slot_bands + plan.map_groups, members, LANES)
+    center_groups = plan.slot_bands * states
     if aligned:
-        packed, upward, downward = pl.pallas_call(
+        packed, turned = pl.pallas_call(
             functools.partial(pack_kernel, plan),
             out_shape=(
-                jax.ShapeDtypeStruct(buffer, bf16),
+                jax.ShapeDtypeStruct((count, center_groups, members, LANES), bf16),
+                jax.ShapeDtypeStruct((states, plan.rows, members, plan.cols), bf16),
+            ),
+            in_specs=[VMEM],
+            out_specs=(VMEM, VMEM),
+            scratch_shapes=[pltpu.VMEM((DEPTH * plan.cols, DEPTH * plan.cols), bf16)],
+            compiler_params=PARAMS,
+            name="pack",
+        )(x)
+    else:
+        packed, side_slots, upward, downward = pack_plain(plan, x)
+    centers = lax.all_to_all(packed, "mem", split_axis=0, concat_axis=0, tiled=True)
+    if aligned:
+        own, upward, downward = pl.pallas_call(
+            functools.partial(sides_kernel, plan),
+            out_shape=(
+                jax.ShapeDtypeStruct((patches,) + strip, bf16),
                 jax.ShapeDtypeStruct(strip, bf16),
                 jax.ShapeDtypeStruct(strip, bf16),
             ),
             in_specs=[VMEM],
             out_specs=(VMEM, VMEM, VMEM),
             scratch_shapes=[
-                pltpu.VMEM((plan.states, plan.rows, plan.members, plan.cols), bf16),
-                pltpu.VMEM((DEPTH * plan.cols, DEPTH * plan.cols), bf16),
-                pltpu.VMEM((plan.states * DEPTH * plan.cols, (patches + 2) * LANES), bf16),
+                pltpu.VMEM((states * DEPTH * plan.cols, (patches + 2) * LANES), bf16),
             ],
             compiler_params=PARAMS,
-            name="pack",
-        )(x)
-    else:
-        packed, upward, downward = pack_plain(plan, x)
+            name="sides",
+        )(turned)
     forward, backward = shifts("col")
     left = lax.ppermute(upward, "col", forward)
     right = lax.ppermute(downward, "col", backward)
@@ -450,51 +511,62 @@
         inverse.reshape(patches, slots),
     )
     if aligned:
-        packed = pl.pallas_call(
+        parts = pl.pallas_call(
             functools.partial(join_kernel, plan),
-            out_shape=jax.ShapeDtypeStruct(buffer, bf16),
+            out_shape=(jax.ShapeDtypeStruct(side_slot[1:], bf16),) * count,
             in_specs=[SMEM, VMEM, VMEM, VMEM, VMEM],
-            out_specs=VMEM,
+            out_specs=(VMEM,) * count,
+            scratch_shapes=[pltpu.VMEM(side_slot, bf16)],
             compiler_params=PARAMS,
             name="join",
-        )((index // patches).reshape(1), packed, maps, left, right)
+        )(where, own, maps, left, right)
+        arrived = [parts[0]] + [
+            lax.ppermute(parts[k], "mem", [(i, i ^ k) for i in range(count)]) for k in range(1, count)
+        ]
     else:
         for b in range(plan.bands):
-            at = slice(b * plan.members, (b + 1) * plan.members)
+            at = slice(b * members, (b + 1) * members)
             for column, extra in ((0, left[at]), (patches - 1, right[at])):
                 for g, position in plan.band_slots(b):
-                    here = position * plan.per_band + plan.states
-                    packed = packed.at[plan.index_of[(g, column)], here].add(extra)
+                    side_slots = side_slots.at[plan.index_of[(g, column)], position].add(extra)
         for i, (g, c) in enumerate(plan.place):
-            piece = jnp.where(index // patches == g, maps[c], 0).reshape(-1, plan.members, LANES)
-            packed = packed.at[i, plan.field :].set(piece)
-    arrived = lax.all_to_all(packed, "mem", split_axis=0, concat_axis=0, tiled=True)
-    group = jnp.asarray([g for g, _ in plan.place], i32)[index]
-    shift = jnp.where(group == 0, 0 if plan.full else 1, 0)
-    where = jnp.stack([group, shift]).astype(i32)
-    if aligned:
-        fields, map_source, map_at = arrived, arrived, plan.field
-        pieces = (count, plan.members)
-    else:
-        fields = arrived[:, : plan.field].transpose(1, 0, 2, 3).reshape(1, plan.field, plan.total, LANES)
-        map_source = arrived[:, plan.field :].reshape(count, 1, 4 * MAP_ROWS, LANES)
-        map_at = 0
-        pieces = (1, plan.total)
-    bands = (patches + 2) * plan.per_band
+            piece = jnp.where(index // patches == g, maps[c], 0).reshape(-1, members, LANES)
+            side_slots = side_slots.at[i, plan.slot_bands :].set(piece)
+        arrived = lax.all_to_all(side_slots, "mem", split_axis=0, concat_axis=0, tiled=True)
+        centers, sides = (
+            a.transpose(1, 0, 2, 3).reshape(1, -1, total, LANES)
+            for a in (centers, arrived[:, : plan.slot_bands])
+        )
+        arrived = [sides, arrived[:, plan.slot_bands :].reshape(count, 1, 4 * MAP_ROWS, LANES)]
+    pieces = (count, members) if aligned else (1, total)
+    bands = patches + 2
+    center_xs, center_avgs = pl.pallas_call(
+        functools.partial(center_kernel, plan),
+        out_shape=(
+            jax.ShapeDtypeStruct((total, bands * states * LANES), bf16),
+            jax.ShapeDtypeStruct((bands * 8, LANES), f32),
+        ),
+        in_specs=[SMEM, VMEM],
+        out_specs=(VMEM, VMEM),
+        compiler_params=PARAMS,
+        name="center",
+    )(where, centers)
+    depth = 3 * (states + 1) * LANES
     analysed = pl.pallas_call(
-        functools.partial(analyse_kernel, plan, map_at),
-        out_shape=jax.ShapeDtypeStruct((pieces[0], patches * plan.states, pieces[1], LANES), bf16),
-        in_specs=[SMEM, VMEM, VMEM],
+        functools.partial(analyse_kernel, plan, aligned),
+        out_shape=jax.ShapeDtypeStruct((pieces[0], patches * states, pieces[1], LANES), bf16),
+        in_specs=[SMEM, VMEM, VMEM] + [VMEM] * len(arrived),
         out_specs=VMEM,
         scratch_shapes=[
-            pltpu.VMEM((plan.total, bands * LANES), bf16),
-            pltpu.VMEM(((patches + 2) * 8, LANES), f32),
-            pltpu.VMEM((patches, plan.total + 16, 3 * plan.per_band * LANES), bf16),
-            pltpu.VMEM((16, 3 * plan.per_band * LANES), f32),
+            pltpu.VMEM((total, bands * LANES), bf16),
+            pltpu.VMEM((8, LANES), f32),
+            pltpu.VMEM((patches, total + 16, depth), bf16),
+            pltpu.VMEM((16, depth), f32),
+            pltpu.VMEM(side_slot if aligned else (8, LANES), bf16),
         ],
         compiler_params=PARAMS,
         name="analyse",
-    )(where, fields, map_source)
+    )(where, center_xs, center_avgs, *arrived)
     if not aligned:
         analysed = analysed.reshape(-1, count, plan.members, LANES).transpose(1, 0, 2, 3)
     returned = lax.all_to_all(analysed, "mem", split_axis=0, concat_axis=0, tiled=True)

time: 76.9 us -> 64.7 us (0.84)
  waiting for transfers between devices: 21.1 us -> 8.89 us
  starting transfers between devices: 10.1 us -> 16.8 us
  local copies, waits for them, and re-layouts: 6.15 us -> 1.25 us
    all_to_all x1, waiting for transfers between devices: 21.1 us -> 0.01 us  [local(): lax.all_to_all(packed, 'mem', split_axis=0, concat_axis=0, tiled=True)]
    ppermute x0 -> x7, starting transfers between devices: none -> 6.63 us  [local(): lax.ppermute(parts[k], 'mem', [(i, i ^ k) for i in range(count)])]
    ppermute x0 -> x7, waiting for transfers between devices: none -> 5.57 us  [local(): lax.ppermute(parts[k], 'mem', [(i, i ^ k) for i in range(count)])]
    unnamed x16 -> x14, local copies, waits for them, and re-layouts: 5.56 us -> 1.25 us
    ppermute x1, waiting for transfers between devices: 0.01 us -> 3.32 us  [local(): right = lax.ppermute(downward, 'col', backward)]
    all_to_all x1, starting transfers between devices: 3.85 us -> 5.34 us  [local(): lax.all_to_all(packed, 'mem', split_axis=0, concat_axis=0, tiled=True)]
    ppermute x1, starting transfers between devices: 4.96 us -> 3.48 us  [local(): left = lax.ppermute(upward, 'col', forward)]
    pallas_call x2 -> x4, Pallas kernels: 12.5 us -> 12.1 us  [the longest x1 10.4 us: local(): pl.pallas_call(functools.partial(analyse_kernel, plan, aligned), out_shap...]
  transfers between devices with their start and end apart: 3 -> 10, of which waited for: 1 -> 5; matrix products, arithmetic and copies ran while one was open for 2% -> 0% of each run, Pallas kernels for 2% -> 5%
where the time goes in v2:
time: 64.7 us; the launch traced here: 64.3 us
  Pallas kernels  19.4 us (30%)
  blocking collectives  17.9 us (28%)
  starting transfers between devices  16.8 us (26%)
  waiting for transfers between devices  8.89 us (14%)
  local copies, waits for them, and re-layouts  1.25 us (2%)
    all_to_all x1, blocking collectives, local(): lax.all_to_all(analysed, 'mem', split_axis=0, concat_axis=0, tiled=True)  17.9 us
    pallas_call x1, Pallas kernels, local(): pl.pallas_call(functools.partial(analyse_kernel, plan, aligned), out_shap...  10.4 us
    ppermute x7, starting transfers between devices, local(): lax.ppermute(parts[k], 'mem', [(i, i ^ k) for i in range(count)])  6.63 us
    ppermute x7, waiting for transfers between devices, local(): lax.ppermute(parts[k], 'mem', [(i, i ^ k) for i in range(count)])  5.57 us
    all_to_all x1, starting transfers between devices, local(): lax.all_to_all(packed, 'mem', split_axis=0, concat_axis=0, tiled=True)  5.34 us
    ppermute x1, starting transfers between devices, local(): left = lax.ppermute(upward, 'col', forward)  3.48 us
    ppermute x1, waiting for transfers between devices, local(): right = lax.ppermute(downward, 'col', backward)  3.32 us
    pallas_call x1, Pallas kernels, local(): pl.pallas_call(functools.partial(pack_kernel, plan), out_shape=(jax.Shape...  2.95 us
  transfers between devices with their start and end apart: 10, of which 5 were waited for; matrix products, arithmetic and copies ran while one was open for 0% of the time, Pallas kernels for 5%

profile of v2, /device:TPU:0, one launch (start us, length us, event | category | flops | bytes accessed | tf_op | source)
XLA Modules:
  0.0 64.3 jit_solution(10341504209257055503)
XLA Ops:
  0.0 1.2 %copy-done = bf16[32,4,32,128]{3,2,1,0:T(8,128)(2,1)S(1)} copy-done((bf16[32,4,32,128]{3,2,1,0:T(8,128)(2,1)S(1)}, bf16[32,4,32,128]{3,2,1,0:T(8,128)(2,1)}, u32[]{:S(2)}) %copy-start) | copy-done | bytes 1048600
  1.2 2.9 %pack.1 = (bf16[8,20,32,128]{3,2,1,0:T(8,128)(2,1)}, bf16[4,32,32,128]{3,2,1,0:T(8,128)(2,1)S(1)}) custom-call(bf16[32,4,32,128]{3,2,1,0:T(8,128)(2,1)S(1)} %copy-done), custom_call_target="tpu_custom_call" | custom-call | tf_op jit(solution)/shard_map/pack/pallas_call | solution.py:463
  4.2 0.0 copy-start.5
  4.2 0.0 copy-start.6
  4.2 5.3 %all-to-all-start = ((bf16[8,20,32,128]{3,2,1,0:T(8,128)(2,1)}), bf16[8,20,32,128]{3,2,1,0:T(8,128)(2,1)S(1)}, u32[]{:S(2)}, u32[]{:S(2)}) async-start(bf16[8,20,32,128]{3,2,1,0:T(8,128)(2,1)} %get-tuple-element.20), calls=%async_computation | async-start | bytes 2621440 | tf_op jit(solution)/shard_map/all_to_all | solution.py:477
  9.6 1.0 %sides.1 = (bf16[4,256,128]{2,1,0:T(8,128)(2,1)S(1)}, bf16[256,128]{1,0:T(8,128)(2,1)S(1)}, bf16[256,128]{1,0:T(8,128)(2,1)S(1)}) custom-call(bf16[4,32,32,128]{3,2,1,0:T(8,128)(2,1)S(1)} %get-tuple-element.23.turned), custom_call_target="tpu_custom_call" | custom-call | tf_op jit(solution)/shard_map/sides/pallas_call | solution.py:479
  10.5 3.5 %collective-permute-start = (bf16[256,128]{1,0:T(8,128)(2,1)S(1)}, bf16[256,128]{1,0:T(8,128)(2,1)S(1)}, u32[]{:S(2)}, u32[]{:S(2)}) collective-permute-start(bf16[256,128]{1,0:T(8,128)(2,1)S(1)} %get-tuple-element.25), channel_id=1, source_target_pairs={{0,1},{1,2},{2,3},{4,5},{5,6},{6,7},{8,9},{9,10},{10,11},{12,13},{... | collective-permute-start | bytes 196616 | tf_op jit(solution)/shard_map/ppermute | solution.py:495
  14.0 1.3 %collective-permute-start.1 = (bf16[256,128]{1,0:T(8,128)(2,1)S(1)}, bf16[256,128]{1,0:T(8,128)(2,1)S(1)}, u32[]{:S(2)}, u32[]{:S(2)}) collective-permute-start(bf16[256,128]{1,0:T(8,128)(2,1)S(1)} %get-tuple-element.26), channel_id=1, source_target_pairs={{1,0},{2,1},{3,2},{5,4},{6,5},{7,6},{9,8},{10,9},{11,10},{13,12},{... | collective-permute-start | bytes 196616 | tf_op jit(solution)/shard_map/ppermute | solution.py:496
  15.3 0.0 copy-done.1
  15.4 1.5 %maps.1.maps_ref = bf16[4,64,128]{2,1,0:T(8,128)(2,1)S(1)} custom-call(s32[1,4]{1,0:T(1,128)S(1)} %copy-done.5, f32[16]{0:T(128)S(1)} %copy-done.6, s32[4,2048]{1,0:T(4,128)S(1)} %bitcast.5, s32[4,2048]{1,0:T(4,128)S(1)} %bitcast.6, f32[4,2048]{1,0:T(4,128)S(1)} %bitcast.7, f32[4,2048]{1,0:T(4,128)S(1)} %bitcast.8), custom_call_target="tpu_custom_call" | custom-call | tf_op jit(solution)/shard_map/maps/pallas_call | solution.py:498
  16.9 0.0 collective-permute-done.left_ref
  16.9 3.3 %collective-permute-done.1.right_ref = bf16[256,128]{1,0:T(8,128)(2,1)S(1)} collective-permute-done((bf16[256,128]{1,0:T(8,128)(2,1)S(1)}, bf16[256,128]{1,0:T(8,128)(2,1)S(1)}, u32[]{:S(2)}, u32[]{:S(2)}) %collective-permute-start.1) | collective-permute-done | bytes 65568 | tf_op jit(solution)/shard_map/ppermute | solution.py:496
  20.2 0.1 join.1
  20.3 0.1 collective-permute-start.2
  20.4 2.1 %collective-permute-start.3 = (bf16[7,32,128]{2,1,0:T(8,128)(2,1)S(1)}, bf16[7,32,128]{2,1,0:T(8,128)(2,1)S(1)}, u32[]{:S(2)}, u32[]{:S(2)}) collective-permute-start(bf16[7,32,128]{2,1,0:T(8,128)(2,1)S(1)} %get-tuple-element.29), channel_id=1, source_target_pairs={{0,8},{4,12},{8,0},{12,4},{16,24},{20,28},{24,16},{28,20},{1,9},{5... | collective-permute-start | bytes 172040 | tf_op jit(solution)/shard_map/ppermute | solution.py:524
  22.5 0.0 collective-permute-start.4
  22.5 1.7 %collective-permute-start.5 = (bf16[7,32,128]{2,1,0:T(8,128)(2,1)S(1)}, bf16[7,32,128]{2,1,0:T(8,128)(2,1)S(1)}, u32[]{:S(2)}, u32[]{:S(2)}) collective-permute-start(bf16[7,32,128]{2,1,0:T(8,128)(2,1)S(1)} %get-tuple-element.31), channel_id=1, source_target_pairs={{0,16},{4,20},{8,24},{12,28},{16,0},{20,4},{24,8},{28,12},{1,17},{... | collective-permute-start | bytes 172040 | tf_op jit(solution)/shard_map/ppermute | solution.py:524
  24.3 0.0 collective-permute-start.6
  24.3 0.0 collective-permute-done.2.rest_1_
  24.3 2.6 %collective-permute-start.7 = (bf16[7,32,128]{2,1,0:T(8,128)(2,1)S(1)}, bf16[7,32,128]{2,1,0:T(8,128)(2,1)S(1)}, u32[]{:S(2)}, u32[]{:S(2)}) collective-permute-start(bf16[7,32,128]{2,1,0:T(8,128)(2,1)S(1)} %get-tuple-element.33), channel_id=1, source_target_pairs={{0,24},{4,28},{8,16},{12,20},{16,8},{20,12},{24,0},{28,4},{1,25},{... | collective-permute-start | bytes 172040 | tf_op jit(solution)/shard_map/ppermute | solution.py:524
  26.9 1.8 %collective-permute-done.3.rest_2_ = bf16[7,32,128]{2,1,0:T(8,128)(2,1)S(1)} collective-permute-done((bf16[7,32,128]{2,1,0:T(8,128)(2,1)S(1)}, bf16[7,32,128]{2,1,0:T(8,128)(2,1)S(1)}, u32[]{:S(2)}, u32[]{:S(2)}) %collective-permute-start.3) | collective-permute-done | bytes 57376 | tf_op jit(solution)/shard_map/ppermute | solution.py:524
  28.6 0.1 collective-permute-start.8
  28.7 0.0 all-to-all-done.x_ref
  28.7 0.6 center.1
  29.3 0.0 collective-permute-done.4.rest_3_
  29.3 0.0 collective-permute-done.5.rest_4_
  29.3 1.3 %collective-permute-done.6.rest_5_ = bf16[7,32,128]{2,1,0:T(8,128)(2,1)S(1)} collective-permute-done((bf16[7,32,128]{2,1,0:T(8,128)(2,1)S(1)}, bf16[7,32,128]{2,1,0:T(8,128)(2,1)S(1)}, u32[]{:S(2)}, u32[]{:S(2)}) %collective-permute-start.6) | collective-permute-done | bytes 57376 | tf_op jit(solution)/shard_map/ppermute | solution.py:524
  30.6 0.8 %collective-permute-done.7.rest_6_ = bf16[7,32,128]{2,1,0:T(8,128)(2,1)S(1)} collective-permute-done((bf16[7,32,128]{2,1,0:T(8,128)(2,1)S(1)}, bf16[7,32,128]{2,1,0:T(8,128)(2,1)S(1)}, u32[]{:S(2)}, u32[]{:S(2)}) %collective-permute-start.7) | collective-permute-done | bytes 57376 | tf_op jit(solution)/shard_map/ppermute | solution.py:524
  31.5 1.7 %collective-permute-done.8.rest_7_ = bf16[7,32,128]{2,1,0:T(8,128)(2,1)S(1)} collective-permute-done((bf16[7,32,128]{2,1,0:T(8,128)(2,1)S(1)}, bf16[7,32,128]{2,1,0:T(8,128)(2,1)S(1)}, u32[]{:S(2)}, u32[]{:S(2)}) %collective-permute-start.8) | collective-permute-done | bytes 57376 | tf_op jit(solution)/shard_map/ppermute | solution.py:524
  33.1 10.4 %analyse.1 = bf16[8,16,32,128]{3,2,1,0:T(8,128)(2,1)S(1)} custom-call(s32[1]{0:T(128)} %bitcast.place_ref, bf16[256,3072]{1,0:T(8,128)(2,1)S(1)} %get-tuple-element.21.xs, f32[48,128]{1,0:T(8,128)S(1)} %get-tuple-element.22.avgs, bf16[7,32,128]{2,1,0:T(8,128)(2,1)S(1)} %get-tuple-element.27.rest_0_, bf16[7,32,128]{2,1,0:T(8,128)(2,1)S(1)} %collective-permute-done.2.rest_1_, ...), custom_call_target="tpu_custom_call" | custom-call | tf_op jit(solution)/shard_map/analyse/pallas_call | solution.py:555
  43.6 17.9 %all_to_all.10.in_ref = bf16[8,16,32,128]{3,2,1,0:T(8,128)(2,1)S(1)} all-to-all(bf16[8,16,32,128]{3,2,1,0:T(8,128)(2,1)S(1)} %analyse.1), channel_id=1, replica_groups=mesh['mem'=8,'col'=4] {'mem'}, dimensions={0} | all-to-all | bytes 2097152 | tf_op jit(solution)/shard_map/all_to_all | solution.py:572
  61.5 2.8 %unpack.1 = bf16[32,4,32,128]{3,2,1,0:T(8,128)(2,1)} custom-call(bf16[8,16,32,128]{3,2,1,0:T(8,128)(2,1)S(1)} %all_to_all.10.in_ref), custom_call_target="tpu_custom_call" | custom-call | tf_op jit(solution)/shard_map/unpack/pallas_call | solution.py:575
  (10 shorter events, 0.0 us)
Async XLA Ops:
  0.0 1.2 %copy-start = (bf16[32,4,32,128]{3,2,1,0:T(8,128)(2,1)S(1)}, bf16[32,4,32,128]{3,2,1,0:T(8,128)(2,1)}, u32[]{:S(2)}) copy-start(bf16[32,4,32,128]{3,2,1,0:T(8,128)(2,1)} %x_ref.1) | copy-start | bytes 3145732
  4.2 11.2 %copy-start.1 = (s32[1,4,2048]{2,1,0:T(4,128)S(1)}, s32[1,4,2048]{2,1,0:T(4,128)}, u32[]{:S(2)}) copy-start(s32[1,4,2048]{2,1,0:T(4,128)} %param.9) | copy-start | bytes 98308
  4.2 11.2 %copy-start.2 = (s32[1,4,2048]{2,1,0:T(4,128)S(1)}, s32[1,4,2048]{2,1,0:T(4,128)}, u32[]{:S(2)}) copy-start(s32[1,4,2048]{2,1,0:T(4,128)} %param.10) | copy-start | bytes 98308
  4.2 11.2 %copy-start.3 = (f32[1,4,2048]{2,1,0:T(4,128)S(1)}, f32[1,4,2048]{2,1,0:T(4,128)}, u32[]{:S(2)}) copy-start(f32[1,4,2048]{2,1,0:T(4,128)} %param.11) | copy-start | bytes 98308
  4.2 11.2 %copy-start.4 = (f32[1,4,2048]{2,1,0:T(4,128)S(1)}, f32[1,4,2048]{2,1,0:T(4,128)}, u32[]{:S(2)}) copy-start(f32[1,4,2048]{2,1,0:T(4,128)} %param.12) | copy-start | bytes 98308
  4.2 11.2 %copy-start.5 = (s32[1,4]{1,0:T(1,128)S(1)}, s32[1,4]{1,0:T(1,128)}, u32[]{:S(2)}) copy-start(s32[1,4]{1,0:T(1,128)} %count_ref.1) | copy-start | bytes 52
  4.2 11.2 %copy-start.6 = (f32[16]{0:T(128)S(1)}, f32[16]{0:T(128)}, u32[]{:S(2)}) copy-start(f32[16]{0:T(128)} %factor_ref.1) | copy-start | bytes 196
  4.2 24.5 %all-to-all-start = ((bf16[8,20,32,128]{3,2,1,0:T(8,128)(2,1)}), bf16[8,20,32,128]{3,2,1,0:T(8,128)(2,1)S(1)}, u32[]{:S(2)}, u32[]{:S(2)}) async-start(bf16[8,20,32,128]{3,2,1,0:T(8,128)(2,1)} %get-tuple-element.20), calls=%async_computation | async-start | bytes 2621440 | tf_op jit(solution)/shard_map/all_to_all | solution.py:477
  10.5 6.3 %collective-permute-start = (bf16[256,128]{1,0:T(8,128)(2,1)S(1)}, bf16[256,128]{1,0:T(8,128)(2,1)S(1)}, u32[]{:S(2)}, u32[]{:S(2)}) collective-permute-start(bf16[256,128]{1,0:T(8,128)(2,1)S(1)} %get-tuple-element.25), channel_id=1, source_target_pairs={{0,1},{1,2},{2,3},{4,5},{5,6},{6,7},{8,9},{9,10},{10,11},{12,13},{... | collective-permute-start | bytes 196616 | tf_op jit(solution)/shard_map/ppermute | solution.py:495
  14.0 6.2 %collective-permute-start.1 = (bf16[256,128]{1,0:T(8,128)(2,1)S(1)}, bf16[256,128]{1,0:T(8,128)(2,1)S(1)}, u32[]{:S(2)}, u32[]{:S(2)}) collective-permute-start(bf16[256,128]{1,0:T(8,128)(2,1)S(1)} %get-tuple-element.26), channel_id=1, source_target_pairs={{1,0},{2,1},{3,2},{5,4},{6,5},{7,6},{9,8},{10,9},{11,10},{13,12},{... | collective-permute-start | bytes 196616 | tf_op jit(solution)/shard_map/ppermute | solution.py:496
  20.3 4.0 %collective-permute-start.2 = (bf16[7,32,128]{2,1,0:T(8,128)(2,1)S(1)}, bf16[7,32,128]{2,1,0:T(8,128)(2,1)S(1)}, u32[]{:S(2)}, u32[]{:S(2)}) collective-permute-start(bf16[7,32,128]{2,1,0:T(8,128)(2,1)S(1)} %get-tuple-element.28), channel_id=1, source_target_pairs={{0,4},{4,0},{8,12},{12,8},{16,20},{20,16},{24,28},{28,24},{1,5},{5... | collective-permute-start | bytes 172040 | tf_op jit(solution)/shard_map/ppermute | solution.py:524
  20.4 8.3 %collective-permute-start.3 = (bf16[7,32,128]{2,1,0:T(8,128)(2,1)S(1)}, bf16[7,32,128]{2,1,0:T(8,128)(2,1)S(1)}, u32[]{:S(2)}, u32[]{:S(2)}) collective-permute-start(bf16[7,32,128]{2,1,0:T(8,128)(2,1)S(1)} %get-tuple-element.29), channel_id=1, source_target_pairs={{0,8},{4,12},{8,0},{12,4},{16,24},{20,28},{24,16},{28,20},{1,9},{5... | collective-permute-start | bytes 172040 | tf_op jit(solution)/shard_map/ppermute | solution.py:524
  22.5 6.9 %collective-permute-start.4 = (bf16[7,32,128]{2,1,0:T(8,128)(2,1)S(1)}, bf16[7,32,128]{2,1,0:T(8,128)(2,1)S(1)}, u32[]{:S(2)}, u32[]{:S(2)}) collective-permute-start(bf16[7,32,128]{2,1,0:T(8,128)(2,1)S(1)} %get-tuple-element.30), channel_id=1, source_target_pairs={{0,12},{4,8},{8,4},{12,0},{16,28},{20,24},{24,20},{28,16},{1,13},{... | collective-permute-start | bytes 172040 | tf_op jit(solution)/shard_map/ppermute | solution.py:524
  22.5 6.8 %collective-permute-start.5 = (bf16[7,32,128]{2,1,0:T(8,128)(2,1)S(1)}, bf16[7,32,128]{2,1,0:T(8,128)(2,1)S(1)}, u32[]{:S(2)}, u32[]{:S(2)}) collective-permute-start(bf16[7,32,128]{2,1,0:T(8,128)(2,1)S(1)} %get-tuple-element.31), channel_id=1, source_target_pairs={{0,16},{4,20},{8,24},{12,28},{16,0},{20,4},{24,8},{28,12},{1,17},{... | collective-permute-start | bytes 172040 | tf_op jit(solution)/shard_map/ppermute | solution.py:524
  24.3 6.4 %collective-permute-start.6 = (bf16[7,32,128]{2,1,0:T(8,128)(2,1)S(1)}, bf16[7,32,128]{2,1,0:T(8,128)(2,1)S(1)}, u32[]{:S(2)}, u32[]{:S(2)}) collective-permute-start(bf16[7,32,128]{2,1,0:T(8,128)(2,1)S(1)} %get-tuple-element.32), channel_id=1, source_target_pairs={{0,20},{4,16},{8,28},{12,24},{16,4},{20,0},{24,12},{28,8},{1,21},{... | collective-permute-start | bytes 172040 | tf_op jit(solution)/shard_map/ppermute | solution.py:524
  24.3 7.2 %collective-permute-start.7 = (bf16[7,32,128]{2,1,0:T(8,128)(2,1)S(1)}, bf16[7,32,128]{2,1,0:T(8,128)(2,1)S(1)}, u32[]{:S(2)}, u32[]{:S(2)}) collective-permute-start(bf16[7,32,128]{2,1,0:T(8,128)(2,1)S(1)} %get-tuple-element.33), channel_id=1, source_target_pairs={{0,24},{4,28},{8,16},{12,20},{16,8},{20,12},{24,0},{28,4},{1,25},{... | collective-permute-start | bytes 172040 | tf_op jit(solution)/shard_map/ppermute | solution.py:524
  28.6 4.5 %collective-permute-start.8 = (bf16[7,32,128]{2,1,0:T(8,128)(2,1)S(1)}, bf16[7,32,128]{2,1,0:T(8,128)(2,1)S(1)}, u32[]{:S(2)}, u32[]{:S(2)}) collective-permute-start(bf16[7,32,128]{2,1,0:T(8,128)(2,1)S(1)} %get-tuple-element.34), channel_id=1, source_target_pairs={{0,28},{4,24},{8,20},{12,16},{16,12},{20,8},{24,4},{28,0},{1,29},{... | collective-permute-start | bytes 172040 | tf_op jit(solution)/shard_map/ppermute | solution.py:524

commit v3 on v2

--- a/solution.py
+++ b/solution.py
@@ -11,6 +11,7 @@
 MARGIN = 4
 ITERS = 4
 LANES = 128
+HALF = 16
 MAP_ROWS = 16
 INFLATION = 1.1
 
@@ -19,7 +20,7 @@
 i32 = jnp.int32
 VMEM = pl.BlockSpec(memory_space=pltpu.VMEM)
 SMEM = pl.BlockSpec(memory_space=pltpu.SMEM)
-PARAMS = pltpu.CompilerParams(vmem_limit_bytes=24 * 1024 * 1024)
+PARAMS = pltpu.CompilerParams(vmem_limit_bytes=14 * 1024 * 1024)
 
 
 def iota(shape, dim):
@@ -82,28 +83,48 @@
     return jnp.where(eighth < MARGIN, low, high)
 
 
-def pack_kernel(plan, x_ref, buf_ref, turned, q_ref):
-    half = 16
-    rows, cols = plan.rows, plan.cols
-    span = half * rows
-    r = iota((span, span), 0)
-    k = iota((span, span), 1)
-    perm = one_hot((r % half == k // rows) & (r // half == k % rows))
-    for s in range(plan.states):
-        for h in range(plan.members // half):
-            piece = x_ref[h * half : (h + 1) * half, s].reshape(span, cols)
-            turned[s, :, h * half : (h + 1) * half, :] = (
-                dot(perm, piece).astype(bf16).reshape(rows, half, cols)
-            )
+def turn_table():
+    r = iota((HALF * HALF, HALF * HALF), 0)
+    k = iota((HALF * HALF, HALF * HALF), 1)
+    return one_hot((r % HALF == k // HALF) & (r // HALF == k % HALF))
+
+
+def lane_table(cols, closing):
     wide = DEPTH * cols
-    r = iota((wide, wide), 0)
-    k = iota((wide, wide), 1)
-    q_ref[...] = one_hot(
+    r = iota((wide, wide), 0 if closing else 1)
+    k = iota((wide, wide), 1 if closing else 0)
+    return one_hot(
         (r // cols == (k % LANES) // SPAN) & (r % cols == (k // LANES) * SPAN + k % SPAN)
     )
+
+
+def turn(table, read, write, first, second):
+    for a in range(0, first, HALF):
+        for b in range(0, second, 2 * HALF):
+            pair = [read(a, b + n * HALF).reshape(HALF * HALF, LANES) for n in range(2)]
+            done = dot(table, jnp.concatenate(pair, axis=1)).astype(bf16)
+            for n in range(2):
+                piece = done[:, n * LANES : (n + 1) * LANES]
+                write(a, b + n * HALF, piece.reshape(HALF, HALF, LANES))
+
+
+def tables_kernel(plan, turn_ref, close_ref):
+    turn_ref[...] = turn_table()
+    close_ref[...] = lane_table(plan.cols, True)
+
+
+def pack_kernel(plan, x_ref, turn_ref, close_ref, buf_ref, turned):
+    table = turn_ref[...]
     m = plan.members
     for s in range(plan.states):
-        center = dot(banded(plan, turned, s), q_ref[...]).astype(bf16)
+        def read(a, b):
+            return x_ref[a : a + HALF, s, b : b + HALF]
+
+        def write(a, b, piece):
+            turned[s, b : b + HALF, a : a + HALF] = piece
+
+        turn(table, read, write, m, plan.rows)
+        center = dot(banded(plan, turned, s), close_ref[...]).astype(bf16)
         for b in range(plan.bands):
             for c in range(plan.patches):
                 value = center[b * m : (b + 1) * m, c * LANES : (c + 1) * LANES]
@@ -234,8 +255,8 @@
         outs[k][...] = buf_ref[index ^ k]
 
 
-def mm3(ah, al, bh, bl):
-    return dot(jnp.concatenate([ah, ah, al], axis=1), jnp.concatenate([bh, bl, bh], axis=0))
+def mm2(a, b):
+    return dot(jnp.concatenate(split2(a), axis=1), jnp.concatenate([b, b], axis=0))
 
 
 def center_of(plan, shift, fields, bands_at, width, xs, avgs):
@@ -266,7 +287,10 @@
         avgs[pl.ds((b + shift) * step, step)] = jnp.concatenate(means, axis=0)
 
 
-def center_kernel(plan, place_ref, x_ref, xs, avgs):
+def center_kernel(plan, place_ref, x_ref, xs, avgs, turn_ref=None, open_ref=None):
+    if open_ref is not None:
+        turn_ref[...] = turn_table()
+        open_ref[...] = lane_table(plan.cols, False)
     shift = plan.shift_of(plan.group_of(place_ref[0]))
     center_of(plan, shift, x_ref, 0, plan.states, xs, avgs)
 
@@ -332,25 +356,34 @@
         norm = jnp.sqrt(jnp.sum(jnp.sum(gram * gram, axis=1, keepdims=True), axis=0, keepdims=True))
         norms.append(norm)
         grams.append(gram / norm)
-    factors, iterates, roots = [], [], []
+    scale = 1.5
+    iterates, rests = [], []
     for q in range(patches):
-        y = split2(grams[q])
-        f = split2(1.5 * eye - 0.5 * grams[q])
-        iterates.append(split2(mm3(*y, *f)))
-        roots.append(f)
+        iterates.append(1.5 * grams[q] - 0.5 * mm2(grams[q], grams[q].astype(bf16)))
+        rests.append(-0.5 * grams[q])
     for sweep in range(1, ITERS):
+        last = sweep + 1 == ITERS
         for q in range(patches):
-            f = split2(1.5 * eye - 0.5 * mm3(*roots[q], *iterates[q]))
-            if sweep + 1 < ITERS:
-                iterates[q] = split2(mm3(*iterates[q], *f))
-                roots[q] = split2(mm3(*roots[q], *f))
-            else:
-                roots[q] = mm3(*roots[q], *f)
+            y = iterates[q].astype(bf16)
+            product = scale * iterates[q] + mm2(rests[q], y)
+            rest = rests[q].astype(bf16)
+            both = mm2(product, rest if last else jnp.concatenate([rest, y], axis=1))
+            rests[q] = 1.5 * rests[q] - 0.5 * (scale * product + both[:, :total])
+            if not last:
+                iterates[q] = 1.5 * iterates[q] - 0.5 * both[:, total:]
+        scale = scale * 1.5
+    roots = [scale * eye + rest for rest in rests]
     for q in range(patches):
         root = roots[q]
         force = jnp.broadcast_to(forcings[q], (8, total))
-        part = jnp.dot(force, root, precision=lax.Precision.HIGHEST, preferred_element_type=f32)
-        move = jnp.dot(part, root, precision=lax.Precision.HIGHEST, preferred_element_type=f32)
+        high, low = split2(root)
+        tall = jnp.concatenate([high, high, low], axis=0)
+
+        def apply(v):
+            h, l = split2(v)
+            return dot(jnp.concatenate([h, l, h], axis=1), tall)
+
+        move = apply(apply(force))
         move = move[:1] / norms[q]
         transform = (jnp.sqrt((total - 1.0) / norms[q]) * root + move).astype(bf16)
         first = (q + 1) * states * LANES
@@ -362,15 +395,9 @@
                 out_ref[n, q * states + s] = value[n * piece_rows : (n + 1) * piece_rows]
 
 
-def unpack_kernel(plan, in_ref, out_ref, q_ref, turned):
-    half = 16
+def unpack_kernel(plan, in_ref, turn_ref, open_ref, out_ref, turned):
     m, rows, cols, states = plan.members, plan.rows, plan.cols, plan.states
-    wide = DEPTH * cols
-    r = iota((wide, wide), 0)
-    k = iota((wide, wide), 1)
-    q_ref[...] = one_hot(
-        (k // cols == (r % LANES) // SPAN) & (k % cols == (r // LANES) * SPAN + r % SPAN)
-    )
+    table = turn_ref[...]
     for s in range(states):
         lhs = []
         for b in range(plan.bands):
@@ -380,20 +407,18 @@
                     [in_ref[plan.index_of[(g, c)], q * states + s] for c in range(plan.patches)], axis=1
                 )
             )
-        opened = dot(jnp.concatenate(lhs, axis=0), q_ref[...]).astype(bf16)
+        opened = dot(jnp.concatenate(lhs, axis=0), open_ref[...]).astype(bf16)
         for b in range(plan.bands):
             for t in range(DEPTH):
                 turned[s, b * DEPTH + t] = opened[b * m : (b + 1) * m, t * cols : (t + 1) * cols]
-    span = half * rows
-    r = iota((span, span), 0)
-    k = iota((span, span), 1)
-    perm = one_hot((k % half == r // rows) & (k // half == r % rows))
-    for s in range(states):
-        for h in range(m // half):
-            piece = turned[s, :, h * half : (h + 1) * half, :].reshape(span, cols)
-            out_ref[h * half : (h + 1) * half, s] = (
-                dot(perm, piece).astype(bf16).reshape(half, rows, cols)
-            )
+
+        def read(a, b):
+            return turned[s, a : a + HALF, b : b + HALF]
+
+        def write(a, b, piece):
+            out_ref[b : b + HALF, s, a : a + HALF] = piece
+
+        turn(table, read, write, rows, m)
 
 
 def shifts(axis):
@@ -454,24 +479,35 @@
     patches = plan.patches
     index = lax.axis_index("mem")
     where = index.reshape(1)
-    aligned = plan.members % 16 == 0
+    aligned = plan.members % (2 * HALF) == 0 and plan.rows % (2 * HALF) == 0
     states, members, total = plan.states, plan.members, plan.total
     strip = (plan.bands * members, LANES)
     side_slot = (count, plan.slot_bands + plan.map_groups, members, LANES)
     center_groups = plan.slot_bands * states
     if aligned:
+        wide = DEPTH * plan.cols
+        tables = (
+            jax.ShapeDtypeStruct((HALF * HALF, HALF * HALF), bf16),
+            jax.ShapeDtypeStruct((wide, wide), bf16),
+        )
+        turning, closing = pl.pallas_call(
+            functools.partial(tables_kernel, plan),
+            out_shape=tables,
+            out_specs=(VMEM, VMEM),
+            compiler_params=PARAMS,
+            name="tables",
+        )()
         packed, turned = pl.pallas_call(
             functools.partial(pack_kernel, plan),
             out_shape=(
                 jax.ShapeDtypeStruct((count, center_groups, members, LANES), bf16),
                 jax.ShapeDtypeStruct((states, plan.rows, members, plan.cols), bf16),
             ),
-            in_specs=[VMEM],
+            in_specs=[VMEM, VMEM, VMEM],
             out_specs=(VMEM, VMEM),
-            scratch_shapes=[pltpu.VMEM((DEPTH * plan.cols, DEPTH * plan.cols), bf16)],
             compiler_params=PARAMS,
             name="pack",
-        )(x)
+        )(x, turning, closing)
     else:
         packed, side_slots, upward, downward = pack_plain(plan, x)
     centers = lax.all_to_all(packed, "mem", split_axis=0, concat_axis=0, tiled=True)
@@ -484,7 +520,7 @@
                 jax.ShapeDtypeStruct(strip, bf16),
             ),
             in_specs=[VMEM],
-            out_specs=(VMEM, VMEM, VMEM),
+            out_specs=(VMEM,) * 3,
             scratch_shapes=[
                 pltpu.VMEM((states * DEPTH * plan.cols, (patches + 2) * LANES), bf16),
             ],
@@ -540,14 +576,15 @@
         arrived = [sides, arrived[:, plan.slot_bands :].reshape(count, 1, 4 * MAP_ROWS, LANES)]
     pieces = (count, members) if aligned else (1, total)
     bands = patches + 2
-    center_xs, center_avgs = pl.pallas_call(
+    center_xs, center_avgs, *opening = pl.pallas_call(
         functools.partial(center_kernel, plan),
         out_shape=(
             jax.ShapeDtypeStruct((total, bands * states * LANES), bf16),
             jax.ShapeDtypeStruct((bands * 8, LANES), f32),
-        ),
+        )
+        + (tables if aligned else ()),
         in_specs=[SMEM, VMEM],
-        out_specs=(VMEM, VMEM),
+        out_specs=(VMEM,) * (4 if aligned else 2),
         compiler_params=PARAMS,
         name="center",
     )(where, centers)
@@ -575,15 +612,12 @@
     return pl.pallas_call(
         functools.partial(unpack_kernel, plan),
         out_shape=jax.ShapeDtypeStruct(x.shape, bf16),
-        in_specs=[VMEM],
+        in_specs=[VMEM, VMEM, VMEM],
         out_specs=VMEM,
-        scratch_shapes=[
-            pltpu.VMEM((DEPTH * plan.cols, DEPTH * plan.cols), bf16),
-            pltpu.VMEM((plan.states, plan.rows, plan.members, plan.cols), bf16),
-        ],
+        scratch_shapes=[pltpu.VMEM((states, plan.rows, members, plan.cols), bf16)],
         compiler_params=PARAMS,
         name="unpack",
-    )(returned)
+    )(returned, *opening)
 
 
 def solution(mesh):

time: 64.7 us -> 61.5 us (0.951)
  Pallas kernels: 19.4 us -> 16.4 us
    pallas_call x1, Pallas kernels: 10.4 us -> 7.69 us  [local(): pl.pallas_call(functools.partial(analyse_kernel, plan, aligned), out_shap...]
where the time goes in v3:
time: 61.5 us; the launch traced here: 61.2 us
  blocking collectives  17.9 us (29%)
  starting transfers between devices  16.7 us (27%)
  Pallas kernels  16.4 us (27%)
  waiting for transfers between devices  8.72 us (14%)
  local copies, waits for them, and re-layouts  1.25 us (2%)
    all_to_all x1, blocking collectives, local(): lax.all_to_all(analysed, 'mem', split_axis=0, concat_axis=0, tiled=True)  17.9 us
    pallas_call x1, Pallas kernels, local(): pl.pallas_call(functools.partial(analyse_kernel, plan, aligned), out_shap...  7.69 us
    ppermute x7, starting transfers between devices, local(): lax.ppermute(parts[k], 'mem', [(i, i ^ k) for i in range(count)])  6.63 us
    ppermute x7, waiting for transfers between devices, local(): lax.ppermute(parts[k], 'mem', [(i, i ^ k) for i in range(count)])  5.4 us
    all_to_all x1, starting transfers between devices, local(): lax.all_to_all(packed, 'mem', split_axis=0, concat_axis=0, tiled=True)  5.34 us
    ppermute x1, starting transfers between devices, local(): left = lax.ppermute(upward, 'col', forward)  3.47 us
    ppermute x1, waiting for transfers between devices, local(): right = lax.ppermute(downward, 'col', backward)  3.32 us
    pallas_call x1, Pallas kernels, local(): pl.pallas_call(functools.partial(unpack_kernel, plan), out_shape=jax.Shap...  2.63 us
  transfers between devices with their start and end apart: 10, of which 5 were waited for; matrix products, arithmetic and copies ran while one was open for 0% of the time, Pallas kernels for 5%

profile of v3, /device:TPU:0, one launch (start us, length us, event | category | flops | bytes accessed | tf_op | source)
XLA Modules:
  0.0 61.2 jit_solution(845419048573832279)
XLA Ops:
  0.0 0.2 tables.1
  0.2 0.0 copy-start
  0.2 1.2 %copy-done = bf16[32,4,32,128]{3,2,1,0:T(8,128)(2,1)S(1)} copy-done((bf16[32,4,32,128]{3,2,1,0:T(8,128)(2,1)S(1)}, bf16[32,4,32,128]{3,2,1,0:T(8,128)(2,1)}, u32[]{:S(2)}) %copy-start) | copy-done | bytes 1048600
  1.5 2.5 %pack.1 = (bf16[8,20,32,128]{3,2,1,0:T(8,128)(2,1)}, bf16[4,32,32,128]{3,2,1,0:T(8,128)(2,1)S(1)}) custom-call(bf16[32,4,32,128]{3,2,1,0:T(8,128)(2,1)S(1)} %copy-done, bf16[256,256]{1,0:T(8,128)(2,1)S(1)} %get-tuple-element.24.turn_ref, bf16[512,512]{1,0:T(8,128)(2,1)S(1)} %get-tuple-element.25.close_ref), custom_call_target="tpu_custom_call" | custom-call | tf_op jit(solution)/shard_map/pack/pallas_call | solution.py:500
  4.0 0.0 copy-start.5
  4.0 0.0 copy-start.6
  4.0 5.3 %all-to-all-start = ((bf16[8,20,32,128]{3,2,1,0:T(8,128)(2,1)}), bf16[8,20,32,128]{3,2,1,0:T(8,128)(2,1)S(1)}, u32[]{:S(2)}, u32[]{:S(2)}) async-start(bf16[8,20,32,128]{3,2,1,0:T(8,128)(2,1)} %get-tuple-element.26), calls=%async_computation | async-start | bytes 2621440 | tf_op jit(solution)/shard_map/all_to_all | solution.py:513
  9.4 1.0 %sides.1 = (bf16[4,256,128]{2,1,0:T(8,128)(2,1)S(1)}, bf16[256,128]{1,0:T(8,128)(2,1)S(1)}, bf16[256,128]{1,0:T(8,128)(2,1)S(1)}) custom-call(bf16[4,32,32,128]{3,2,1,0:T(8,128)(2,1)S(1)} %get-tuple-element.29.turned), custom_call_target="tpu_custom_call" | custom-call | tf_op jit(solution)/shard_map/sides/pallas_call | solution.py:515
  10.4 3.5 %collective-permute-start = (bf16[256,128]{1,0:T(8,128)(2,1)S(1)}, bf16[256,128]{1,0:T(8,128)(2,1)S(1)}, u32[]{:S(2)}, u32[]{:S(2)}) collective-permute-start(bf16[256,128]{1,0:T(8,128)(2,1)S(1)} %get-tuple-element.31), channel_id=1, source_target_pairs={{0,1},{1,2},{2,3},{4,5},{5,6},{6,7},{8,9},{9,10},{10,11},{12,13},{... | collective-permute-start | bytes 196616 | tf_op jit(solution)/shard_map/ppermute | solution.py:531
  13.9 1.3 %collective-permute-start.1 = (bf16[256,128]{1,0:T(8,128)(2,1)S(1)}, bf16[256,128]{1,0:T(8,128)(2,1)S(1)}, u32[]{:S(2)}, u32[]{:S(2)}) collective-permute-start(bf16[256,128]{1,0:T(8,128)(2,1)S(1)} %get-tuple-element.32), channel_id=1, source_target_pairs={{1,0},{2,1},{3,2},{5,4},{6,5},{7,6},{9,8},{10,9},{11,10},{13,12},{... | collective-permute-start | bytes 196616 | tf_op jit(solution)/shard_map/ppermute | solution.py:532
  15.2 1.5 %maps.1.maps_ref = bf16[4,64,128]{2,1,0:T(8,128)(2,1)S(1)} custom-call(s32[1,4]{1,0:T(1,128)S(1)} %copy-done.5, f32[16]{0:T(128)S(1)} %copy-done.6, s32[4,2048]{1,0:T(4,128)S(1)} %bitcast.5, s32[4,2048]{1,0:T(4,128)S(1)} %bitcast.6, f32[4,2048]{1,0:T(4,128)S(1)} %bitcast.7, f32[4,2048]{1,0:T(4,128)S(1)} %bitcast.8), custom_call_target="tpu_custom_call" | custom-call | tf_op jit(solution)/shard_map/maps/pallas_call | solution.py:534
  16.7 0.0 collective-permute-done.left_ref
  16.7 3.3 %collective-permute-done.1.right_ref = bf16[256,128]{1,0:T(8,128)(2,1)S(1)} collective-permute-done((bf16[256,128]{1,0:T(8,128)(2,1)S(1)}, bf16[256,128]{1,0:T(8,128)(2,1)S(1)}, u32[]{:S(2)}, u32[]{:S(2)}) %collective-permute-start.1) | collective-permute-done | bytes 65568 | tf_op jit(solution)/shard_map/ppermute | solution.py:532
  20.0 0.1 join.1
  20.1 0.1 collective-permute-start.2
  20.2 2.1 %collective-permute-start.3 = (bf16[7,32,128]{2,1,0:T(8,128)(2,1)S(1)}, bf16[7,32,128]{2,1,0:T(8,128)(2,1)S(1)}, u32[]{:S(2)}, u32[]{:S(2)}) collective-permute-start(bf16[7,32,128]{2,1,0:T(8,128)(2,1)S(1)} %get-tuple-element.35), channel_id=1, source_target_pairs={{0,8},{4,12},{8,0},{12,4},{16,24},{20,28},{24,16},{28,20},{1,9},{5... | collective-permute-start | bytes 172040 | tf_op jit(solution)/shard_map/ppermute | solution.py:560
  22.3 0.0 collective-permute-start.4
  22.3 1.7 %collective-permute-start.5 = (bf16[7,32,128]{2,1,0:T(8,128)(2,1)S(1)}, bf16[7,32,128]{2,1,0:T(8,128)(2,1)S(1)}, u32[]{:S(2)}, u32[]{:S(2)}) collective-permute-start(bf16[7,32,128]{2,1,0:T(8,128)(2,1)S(1)} %get-tuple-element.37), channel_id=1, source_target_pairs={{0,16},{4,20},{8,24},{12,28},{16,0},{20,4},{24,8},{28,12},{1,17},{... | collective-permute-start | bytes 172040 | tf_op jit(solution)/shard_map/ppermute | solution.py:560
  24.1 0.0 collective-permute-start.6
  24.1 0.0 collective-permute-done.2.rest_1_
  24.1 2.6 %collective-permute-start.7 = (bf16[7,32,128]{2,1,0:T(8,128)(2,1)S(1)}, bf16[7,32,128]{2,1,0:T(8,128)(2,1)S(1)}, u32[]{:S(2)}, u32[]{:S(2)}) collective-permute-start(bf16[7,32,128]{2,1,0:T(8,128)(2,1)S(1)} %get-tuple-element.39), channel_id=1, source_target_pairs={{0,24},{4,28},{8,16},{12,20},{16,8},{20,12},{24,0},{28,4},{1,25},{... | collective-permute-start | bytes 172040 | tf_op jit(solution)/shard_map/ppermute | solution.py:560
  26.7 1.8 %collective-permute-done.3.rest_2_ = bf16[7,32,128]{2,1,0:T(8,128)(2,1)S(1)} collective-permute-done((bf16[7,32,128]{2,1,0:T(8,128)(2,1)S(1)}, bf16[7,32,128]{2,1,0:T(8,128)(2,1)S(1)}, u32[]{:S(2)}, u32[]{:S(2)}) %collective-permute-start.3) | collective-permute-done | bytes 57376 | tf_op jit(solution)/shard_map/ppermute | solution.py:560
  28.5 0.1 collective-permute-start.8
  28.5 0.0 all-to-all-done.x_ref
  28.5 0.8 %center.1 = (bf16[256,3072]{1,0:T(8,128)(2,1)S(1)}, f32[48,128]{1,0:T(8,128)S(1)}, bf16[256,256]{1,0:T(8,128)(2,1)S(1)}, bf16[512,512]{1,0:T(8,128)(2,1)S(1)}) custom-call(s32[1]{0:T(128)} %bitcast.place_ref, bf16[8,20,32,128]{3,2,1,0:T(8,128)(2,1)S(1)} %all-to-all-done.x_ref), custom_call_target="tpu_custom_call" | custom-call | tf_op jit(solution)/shard_map/center/pallas_call | solution.py:579
  29.3 0.0 collective-permute-done.4.rest_3_
  29.4 1.1 %collective-permute-done.6.rest_5_ = bf16[7,32,128]{2,1,0:T(8,128)(2,1)S(1)} collective-permute-done((bf16[7,32,128]{2,1,0:T(8,128)(2,1)S(1)}, bf16[7,32,128]{2,1,0:T(8,128)(2,1)S(1)}, u32[]{:S(2)}, u32[]{:S(2)}) %collective-permute-start.6) | collective-permute-done | bytes 57376 | tf_op jit(solution)/shard_map/ppermute | solution.py:560
  30.4 0.8 %collective-permute-done.7.rest_6_ = bf16[7,32,128]{2,1,0:T(8,128)(2,1)S(1)} collective-permute-done((bf16[7,32,128]{2,1,0:T(8,128)(2,1)S(1)}, bf16[7,32,128]{2,1,0:T(8,128)(2,1)S(1)}, u32[]{:S(2)}, u32[]{:S(2)}) %collective-permute-start.7) | collective-permute-done | bytes 57376 | tf_op jit(solution)/shard_map/ppermute | solution.py:560
  31.3 1.7 %collective-permute-done.8.rest_7_ = bf16[7,32,128]{2,1,0:T(8,128)(2,1)S(1)} collective-permute-done((bf16[7,32,128]{2,1,0:T(8,128)(2,1)S(1)}, bf16[7,32,128]{2,1,0:T(8,128)(2,1)S(1)}, u32[]{:S(2)}, u32[]{:S(2)}) %collective-permute-start.8) | collective-permute-done | bytes 57376 | tf_op jit(solution)/shard_map/ppermute | solution.py:560
  33.0 7.7 %analyse.1 = bf16[8,16,32,128]{3,2,1,0:T(8,128)(2,1)S(1)} custom-call(s32[1]{0:T(128)} %bitcast.place_ref, bf16[256,3072]{1,0:T(8,128)(2,1)S(1)} %get-tuple-element.27.xs, f32[48,128]{1,0:T(8,128)S(1)} %get-tuple-element.28.avgs, bf16[7,32,128]{2,1,0:T(8,128)(2,1)S(1)} %get-tuple-element.33.rest_0_, bf16[7,32,128]{2,1,0:T(8,128)(2,1)S(1)} %collective-permute-done.2.rest_1_, ...), custom_call_target="tpu_custom_call" | custom-call | tf_op jit(solution)/shard_map/analyse/pallas_call | solution.py:592
  40.7 17.9 %all_to_all.10.in_ref = bf16[8,16,32,128]{3,2,1,0:T(8,128)(2,1)S(1)} all-to-all(bf16[8,16,32,128]{3,2,1,0:T(8,128)(2,1)S(1)} %analyse.1), channel_id=1, replica_groups=mesh['mem'=8,'col'=4] {'mem'}, dimensions={0} | all-to-all | bytes 2097152 | tf_op jit(solution)/shard_map/all_to_all | solution.py:609
  58.6 2.6 %unpack.1 = bf16[32,4,32,128]{3,2,1,0:T(8,128)(2,1)} custom-call(bf16[8,16,32,128]{3,2,1,0:T(8,128)(2,1)S(1)} %all_to_all.10.in_ref, bf16[256,256]{1,0:T(8,128)(2,1)S(1)} %get-tuple-element.41.turn_ref, bf16[512,512]{1,0:T(8,128)(2,1)S(1)} %get-tuple-element.42.open_ref), custom_call_target="tpu_custom_call" | custom-call | tf_op jit(solution)/shard_map/unpack/pallas_call | solution.py:612
  (11 shorter events, 0.0 us)
Async XLA Ops:
  0.2 1.2 %copy-start = (bf16[32,4,32,128]{3,2,1,0:T(8,128)(2,1)S(1)}, bf16[32,4,32,128]{3,2,1,0:T(8,128)(2,1)}, u32[]{:S(2)}) copy-start(bf16[32,4,32,128]{3,2,1,0:T(8,128)(2,1)} %x_ref.1) | copy-start | bytes 3145732
  4.0 11.2 %copy-start.1 = (s32[1,4,2048]{2,1,0:T(4,128)S(1)}, s32[1,4,2048]{2,1,0:T(4,128)}, u32[]{:S(2)}) copy-start(s32[1,4,2048]{2,1,0:T(4,128)} %param.9) | copy-start | bytes 98308
  4.0 11.2 %copy-start.2 = (s32[1,4,2048]{2,1,0:T(4,128)S(1)}, s32[1,4,2048]{2,1,0:T(4,128)}, u32[]{:S(2)}) copy-start(s32[1,4,2048]{2,1,0:T(4,128)} %param.10) | copy-start | bytes 98308
  4.0 11.2 %copy-start.3 = (f32[1,4,2048]{2,1,0:T(4,128)S(1)}, f32[1,4,2048]{2,1,0:T(4,128)}, u32[]{:S(2)}) copy-start(f32[1,4,2048]{2,1,0:T(4,128)} %param.11) | copy-start | bytes 98308
  4.0 11.2 %copy-start.4 = (f32[1,4,2048]{2,1,0:T(4,128)S(1)}, f32[1,4,2048]{2,1,0:T(4,128)}, u32[]{:S(2)}) copy-start(f32[1,4,2048]{2,1,0:T(4,128)} %param.12) | copy-start | bytes 98308
  4.0 11.2 %copy-start.5 = (s32[1,4]{1,0:T(1,128)S(1)}, s32[1,4]{1,0:T(1,128)}, u32[]{:S(2)}) copy-start(s32[1,4]{1,0:T(1,128)} %count_ref.1) | copy-start | bytes 52
  4.0 11.2 %copy-start.6 = (f32[16]{0:T(128)S(1)}, f32[16]{0:T(128)}, u32[]{:S(2)}) copy-start(f32[16]{0:T(128)} %factor_ref.1) | copy-start | bytes 196
  4.0 24.5 %all-to-all-start = ((bf16[8,20,32,128]{3,2,1,0:T(8,128)(2,1)}), bf16[8,20,32,128]{3,2,1,0:T(8,128)(2,1)S(1)}, u32[]{:S(2)}, u32[]{:S(2)}) async-start(bf16[8,20,32,128]{3,2,1,0:T(8,128)(2,1)} %get-tuple-element.26), calls=%async_computation | async-start | bytes 2621440 | tf_op jit(solution)/shard_map/all_to_all | solution.py:513
  10.4 6.3 %collective-permute-start = (bf16[256,128]{1,0:T(8,128)(2,1)S(1)}, bf16[256,128]{1,0:T(8,128)(2,1)S(1)}, u32[]{:S(2)}, u32[]{:S(2)}) collective-permute-start(bf16[256,128]{1,0:T(8,128)(2,1)S(1)} %get-tuple-element.31), channel_id=1, source_target_pairs={{0,1},{1,2},{2,3},{4,5},{5,6},{6,7},{8,9},{9,10},{10,11},{12,13},{... | collective-permute-start | bytes 196616 | tf_op jit(solution)/shard_map/ppermute | solution.py:531
  13.9 6.2 %collective-permute-start.1 = (bf16[256,128]{1,0:T(8,128)(2,1)S(1)}, bf16[256,128]{1,0:T(8,128)(2,1)S(1)}, u32[]{:S(2)}, u32[]{:S(2)}) collective-permute-start(bf16[256,128]{1,0:T(8,128)(2,1)S(1)} %get-tuple-element.32), channel_id=1, source_target_pairs={{1,0},{2,1},{3,2},{5,4},{6,5},{7,6},{9,8},{10,9},{11,10},{13,12},{... | collective-permute-start | bytes 196616 | tf_op jit(solution)/shard_map/ppermute | solution.py:532
  20.1 4.0 %collective-permute-start.2 = (bf16[7,32,128]{2,1,0:T(8,128)(2,1)S(1)}, bf16[7,32,128]{2,1,0:T(8,128)(2,1)S(1)}, u32[]{:S(2)}, u32[]{:S(2)}) collective-permute-start(bf16[7,32,128]{2,1,0:T(8,128)(2,1)S(1)} %get-tuple-element.34), channel_id=1, source_target_pairs={{0,4},{4,0},{8,12},{12,8},{16,20},{20,16},{24,28},{28,24},{1,5},{5... | collective-permute-start | bytes 172040 | tf_op jit(solution)/shard_map/ppermute | solution.py:560
  20.2 8.3 %collective-permute-start.3 = (bf16[7,32,128]{2,1,0:T(8,128)(2,1)S(1)}, bf16[7,32,128]{2,1,0:T(8,128)(2,1)S(1)}, u32[]{:S(2)}, u32[]{:S(2)}) collective-permute-start(bf16[7,32,128]{2,1,0:T(8,128)(2,1)S(1)} %get-tuple-element.35), channel_id=1, source_target_pairs={{0,8},{4,12},{8,0},{12,4},{16,24},{20,28},{24,16},{28,20},{1,9},{5... | collective-permute-start | bytes 172040 | tf_op jit(solution)/shard_map/ppermute | solution.py:560
  22.3 7.1 %collective-permute-start.4 = (bf16[7,32,128]{2,1,0:T(8,128)(2,1)S(1)}, bf16[7,32,128]{2,1,0:T(8,128)(2,1)S(1)}, u32[]{:S(2)}, u32[]{:S(2)}) collective-permute-start(bf16[7,32,128]{2,1,0:T(8,128)(2,1)S(1)} %get-tuple-element.36), channel_id=1, source_target_pairs={{0,12},{4,8},{8,4},{12,0},{16,28},{20,24},{24,20},{28,16},{1,13},{... | collective-permute-start | bytes 172040 | tf_op jit(solution)/shard_map/ppermute | solution.py:560
  22.3 7.0 %collective-permute-start.5 = (bf16[7,32,128]{2,1,0:T(8,128)(2,1)S(1)}, bf16[7,32,128]{2,1,0:T(8,128)(2,1)S(1)}, u32[]{:S(2)}, u32[]{:S(2)}) collective-permute-start(bf16[7,32,128]{2,1,0:T(8,128)(2,1)S(1)} %get-tuple-element.37), channel_id=1, source_target_pairs={{0,16},{4,20},{8,24},{12,28},{16,0},{20,4},{24,8},{28,12},{1,17},{... | collective-permute-start | bytes 172040 | tf_op jit(solution)/shard_map/ppermute | solution.py:560
  24.1 6.4 %collective-permute-start.6 = (bf16[7,32,128]{2,1,0:T(8,128)(2,1)S(1)}, bf16[7,32,128]{2,1,0:T(8,128)(2,1)S(1)}, u32[]{:S(2)}, u32[]{:S(2)}) collective-permute-start(bf16[7,32,128]{2,1,0:T(8,128)(2,1)S(1)} %get-tuple-element.38), channel_id=1, source_target_pairs={{0,20},{4,16},{8,28},{12,24},{16,4},{20,0},{24,12},{28,8},{1,21},{... | collective-permute-start | bytes 172040 | tf_op jit(solution)/shard_map/ppermute | solution.py:560
  24.1 7.2 %collective-permute-start.7 = (bf16[7,32,128]{2,1,0:T(8,128)(2,1)S(1)}, bf16[7,32,128]{2,1,0:T(8,128)(2,1)S(1)}, u32[]{:S(2)}, u32[]{:S(2)}) collective-permute-start(bf16[7,32,128]{2,1,0:T(8,128)(2,1)S(1)} %get-tuple-element.39), channel_id=1, source_target_pairs={{0,24},{4,28},{8,16},{12,20},{16,8},{20,12},{24,0},{28,4},{1,25},{... | collective-permute-start | bytes 172040 | tf_op jit(solution)/shard_map/ppermute | solution.py:560
  28.5 4.5 %collective-permute-start.8 = (bf16[7,32,128]{2,1,0:T(8,128)(2,1)S(1)}, bf16[7,32,128]{2,1,0:T(8,128)(2,1)S(1)}, u32[]{:S(2)}, u32[]{:S(2)}) collective-permute-start(bf16[7,32,128]{2,1,0:T(8,128)(2,1)S(1)} %get-tuple-element.40), channel_id=1, source_target_pairs={{0,28},{4,24},{8,20},{12,16},{16,12},{20,8},{24,4},{28,0},{1,29},{... | collective-permute-start | bytes 172040 | tf_op jit(solution)/shard_map/ppermute | solution.py:560

commit v4 on v3

--- a/solution.py
+++ b/solution.py
@@ -36,7 +36,7 @@
 
 
 class Plan:
-    def __init__(self, x_shape, count, states):
+    def __init__(self, x_shape, count):
         self.members, self.states, self.rows, self.cols = x_shape
         self.count = count
         self.total = self.members * count
@@ -52,11 +52,12 @@
             self.place = [(i // self.patches, i % self.patches) for i in range(count)]
         self.slot_bands = self.patches + min(2, self.groups - 1) if self.groups > 1 else self.patches
         self.full = self.slot_bands == self.patches + 2
-        self.per_band = self.states + 1
-        self.field = self.slot_bands * self.per_band
         self.map_groups = 4 * MAP_ROWS // self.members
-        self.slot = self.field + self.map_groups
         self.index_of = {p: i for i, p in enumerate(self.place)}
+        self.aligned = self.members % (2 * HALF) == 0 and self.rows % (2 * HALF) == 0
+        self.aligned = self.aligned and count > 1 and count & (count - 1) == 0
+        self.pair = self.aligned and self.groups == 2
+        self.center_bands = self.patches if self.pair else self.slot_bands
 
     def group_of(self, index):
         return sum(jnp.where(index == i, g, 0) for i, (g, _) in enumerate(self.place))
@@ -75,8 +76,13 @@
             if 0 <= band - self.first_band(g) < self.slot_bands
         ]
 
-
-def side_source(lane, column, cols):
+    def center_slots(self, band):
+        if self.pair:
+            return [(band // self.patches, band % self.patches)]
+        return self.band_slots(band)
+
+
+def side_source(lane, column):
     eighth = lane % (2 * MARGIN)
     low = column * SPAN - MARGIN + eighth
     high = column * SPAN + SPAN + eighth - MARGIN
@@ -128,7 +134,7 @@
         for b in range(plan.bands):
             for c in range(plan.patches):
                 value = center[b * m : (b + 1) * m, c * LANES : (c + 1) * LANES]
-                for g, position in plan.band_slots(b):
+                for g, position in plan.center_slots(b):
                     buf_ref[plan.index_of[(g, c)], position * plan.states + s] = value
     if plan.full:
         zero = jnp.zeros((plan.members, LANES), bf16)
@@ -157,7 +163,7 @@
     column = out // LANES
     lane = out % LANES
     eighth = lane % (2 * MARGIN)
-    source = side_source(lane, column, cols)
+    source = side_source(lane, column)
     to_up = (column == plan.patches) & (eighth < MARGIN)
     to_down = (column == plan.patches + 1) & (eighth >= MARGIN)
     source = jnp.where(column < plan.patches, source, -1)
@@ -251,21 +257,29 @@
         piece = jnp.where(index // plan.patches == g, maps_ref[c], jnp.zeros_like(maps_ref[c]))
         for n in range(plan.map_groups):
             buf_ref[i, plan.slot_bands + n] = piece[n * m : (n + 1) * m]
-    for k in range(plan.count):
-        outs[k][...] = buf_ref[index ^ k]
+    own_half, other_half, _ = outs
+    for k in range(plan.count // 2):
+        own_half[k] = buf_ref[index ^ (2 * k)]
+        other_half[k] = buf_ref[index ^ (2 * k + 1)]
+
+
+def merge_kernel(own_ref, other_ref, *outs):
+    for k, out in enumerate(outs):
+        out[0] = own_ref[k]
+        out[1] = other_ref[k]
 
 
 def mm2(a, b):
     return dot(jnp.concatenate(split2(a), axis=1), jnp.concatenate([b, b], axis=0))
 
 
-def center_of(plan, shift, fields, bands_at, width, xs, avgs):
+def center_of(plan, shift, fields, count, width, xs, avgs):
     sources = fields.shape[0]
     total, patches = plan.total, plan.patches
     step = 8 if width > 1 else 1
-    if not plan.full:
+    if count < patches + 2:
         edges = (0, patches + 1)
-        if plan.slot_bands > patches:
+        if count > patches:
             edges = (jnp.where(shift == 1, 0, patches + 1),)
         for edge in edges:
             lanes = pl.ds(edge * width * LANES, width * LANES)
@@ -273,43 +287,73 @@
                 lanes = pl.ds(pl.multiple_of(edge * width * LANES, LANES), width * LANES)
             xs[:, lanes] = jnp.zeros((total, width * LANES), bf16)
             avgs[pl.ds(edge * step, step)] = jnp.zeros((step, LANES), f32)
-    for b in range(plan.slot_bands):
+    for b in range(count):
         means = []
         for inner in range(width):
-            at = bands_at + b * width + inner
+            at = b * width + inner
             raw = jnp.concatenate([fields[n, at] for n in range(sources)], axis=0).astype(f32)
             mean = jnp.sum(raw, axis=0, keepdims=True) / total
             means.append(mean)
-            lanes = pl.multiple_of(((shift + b) * width + inner) * LANES, LANES)
+            lanes = ((shift + b) * width + inner) * LANES
+            if not isinstance(lanes, int):
+                lanes = pl.multiple_of(lanes, LANES)
             xs[:, pl.ds(lanes, LANES)] = (raw - mean).astype(bf16)
         if width > 1:
             means.append(jnp.zeros((step - width, LANES), f32))
         avgs[pl.ds((b + shift) * step, step)] = jnp.concatenate(means, axis=0)
 
 
-def center_kernel(plan, place_ref, x_ref, xs, avgs, turn_ref=None, open_ref=None):
+def center_kernel(plan, place_ref, x_ref, xs, avgs, turn_ref=None, open_ref=None, send_ref=None):
     if open_ref is not None:
         turn_ref[...] = turn_table()
         open_ref[...] = lane_table(plan.cols, False)
-    shift = plan.shift_of(plan.group_of(place_ref[0]))
-    center_of(plan, shift, x_ref, 0, plan.states, xs, avgs)
+    if send_ref is not None:
+        near = jnp.where(plan.group_of(place_ref[0]) == 0, plan.patches - 1, 0)
+        for n in range(x_ref.shape[0]):
+            for s in range(plan.states):
+                send_ref[n, s] = x_ref[n, near * plan.states + s]
+    shift = 1 if plan.pair else plan.shift_of(plan.group_of(place_ref[0]))
+    center_of(plan, shift, x_ref, plan.center_bands, plan.states, xs, avgs)
 
 
 def analyse_kernel(
     plan, relative, place_ref, xs, avgs, *rest
 ):
-    *pieces, out_ref, side_xs, side_avgs, scaled, lead, gathered = rest
+    *pieces, out_ref, side_xs, side_avgs, scaled, lead, gathered, edge_xs, edge_avgs = rest
 
     total, states, patches = plan.total, plan.states, plan.patches
     sources, _, piece_rows, _ = out_ref.shape
     group = plan.group_of(place_ref[0])
     if relative:
         for k in range(plan.count):
-            gathered[place_ref[0] ^ k] = pieces[k][...]
+            gathered[place_ref[0] ^ k] = pieces[k // 2][k % 2]
+    if plan.pair:
+        near = pieces[-1]
+        wide = states * LANES
+        at = pl.multiple_of(jnp.where(group == 0, wide, 0), LANES)
+        edge_xs[:, pl.ds(pl.multiple_of(wide - at, LANES), wide)] = jnp.zeros((total, wide), bf16)
+        edge_avgs[...] = jnp.zeros_like(edge_avgs)
+        means = []
+        for s in range(states):
+            raw = jnp.concatenate([near[n, s] for n in range(near.shape[0])], axis=0).astype(f32)
+            means.append(jnp.sum(raw, axis=0, keepdims=True) / total)
+            edge_xs[:, pl.ds(pl.multiple_of(at + s * LANES, LANES), LANES)] = (
+                raw - means[-1]
+            ).astype(bf16)
+        means.append(jnp.zeros((8 - states, LANES), f32))
+        edge_avgs[pl.ds(jnp.where(group == 0, 8, 0), 8)] = jnp.concatenate(means, axis=0)
+
+    def block(band):
+        if plan.pair and band in (0, patches + 1):
+            end = int(band > 0)
+            return edge_xs, end * states * LANES, edge_avgs, end * 8
+        return xs, band * states * LANES, avgs, band * 8
+
+    if relative:
         side_ref, maps_ref, map_at = gathered, gathered, plan.slot_bands
     else:
         (side_ref, maps_ref), map_at = pieces, 0
-    center_of(plan, plan.shift_of(group), side_ref, 0, 1, side_xs, side_avgs)
+    center_of(plan, plan.shift_of(group), side_ref, plan.slot_bands, 1, side_xs, side_avgs)
     eye = jnp.where(iota((total, total), 0) == iota((total, total), 1), 1.0, 0.0)
     grams, forcings, norms = [], [], []
     for q in range(patches):
@@ -323,10 +367,10 @@
         lead[...] = jnp.zeros_like(lead)
         for at in range(3 * (states + 1)):
             if at < 3 * states:
-                lanes = (q * states + at) * LANES
-                source = xs[:, lanes : lanes + LANES]
-                row = (q + at // states) * 8 + at % states
-                mean = avgs[row : row + 1]
+                band_xs, lanes, band_avgs, row = block(q + at // states)
+                lanes, row = lanes + at % states * LANES, row + at % states
+                source = band_xs[:, lanes : lanes + LANES]
+                mean = band_avgs[row : row + 1]
             else:
                 row = q + at - 3 * states
                 source = side_xs[:, row * LANES : (row + 1) * LANES]
@@ -340,14 +384,12 @@
                 lead[part : part + 1, here] = high
                 v = v - high
         scaled[q, total:] = lead[...].astype(bf16)
-        first = q * states * LANES
-        window = jnp.concatenate(
-            [
-                xs[:, first : first + 3 * states * LANES],
-                side_xs[:, q * LANES : (q + 3) * LANES],
-            ],
-            axis=1,
-        )
+        window = []
+        for band in range(q, q + 3):
+            band_xs, lanes, _, _ = block(band)
+            window.append(band_xs[:, lanes : lanes + states * LANES])
+        window.append(side_xs[:, q * LANES : (q + 3) * LANES])
+        window = jnp.concatenate(window, axis=1)
         both = lax.dot_general(
             scaled[q], window, (((1,), (1,)), ((), ())), preferred_element_type=f32
         )
@@ -475,15 +517,15 @@
 
 def local(x, tally, cells, classes, readings, inverse, factors):
     count = lax.axis_size("mem")
-    plan = Plan(x.shape, count, x.shape[1])
+    plan = Plan(x.shape, count)
     patches = plan.patches
     index = lax.axis_index("mem")
     where = index.reshape(1)
-    aligned = plan.members % (2 * HALF) == 0 and plan.rows % (2 * HALF) == 0
+    aligned = plan.aligned
     states, members, total = plan.states, plan.members, plan.total
     strip = (plan.bands * members, LANES)
     side_slot = (count, plan.slot_bands + plan.map_groups, members, LANES)
-    center_groups = plan.slot_bands * states
+    center_groups = plan.center_bands * states
     if aligned:
         wide = DEPTH * plan.cols
         tables = (
@@ -547,18 +589,30 @@
         inverse.reshape(patches, slots),
     )
     if aligned:
-        parts = pl.pallas_call(
+        pairs = count // 2
+        half = jax.ShapeDtypeStruct((pairs,) + side_slot[1:], bf16)
+        own_half, other_half = pl.pallas_call(
             functools.partial(join_kernel, plan),
-            out_shape=(jax.ShapeDtypeStruct(side_slot[1:], bf16),) * count,
+            out_shape=(half, half),
             in_specs=[SMEM, VMEM, VMEM, VMEM, VMEM],
-            out_specs=(VMEM,) * count,
+            out_specs=(VMEM, VMEM),
             scratch_shapes=[pltpu.VMEM(side_slot, bf16)],
             compiler_params=PARAMS,
             name="join",
         )(where, own, maps, left, right)
-        arrived = [parts[0]] + [
-            lax.ppermute(parts[k], "mem", [(i, i ^ k) for i in range(count)]) for k in range(1, count)
-        ]
+        other_half = lax.ppermute(other_half, "mem", [(i, i ^ 1) for i in range(count)])
+        parts = pl.pallas_call(
+            merge_kernel,
+            out_shape=(jax.ShapeDtypeStruct((2,) + side_slot[1:], bf16),) * pairs,
+            in_specs=[VMEM, VMEM],
+            out_specs=(VMEM,) * pairs,
+            compiler_params=PARAMS,
+            name="merge",
+        )(own_half, other_half)
+        arrived = [parts[0]]
+        for k in range(1, pairs):
+            pairing = [(i, i ^ (2 * k)) for i in range(count)]
+            arrived.append(lax.ppermute(parts[k], "mem", pairing))
     else:
         for b in range(plan.bands):
             at = slice(b * members, (b + 1) * members)
@@ -582,12 +636,16 @@
             jax.ShapeDtypeStruct((total, bands * states * LANES), bf16),
             jax.ShapeDtypeStruct((bands * 8, LANES), f32),
         )
-        + (tables if aligned else ()),
+        + (tables if aligned else ())
+        + ((jax.ShapeDtypeStruct((count, states, members, LANES), bf16),) if plan.pair else ()),
         in_specs=[SMEM, VMEM],
-        out_specs=(VMEM,) * (4 if aligned else 2),
+        out_specs=(VMEM,) * (2 + 2 * aligned + plan.pair),
         compiler_params=PARAMS,
         name="center",
     )(where, centers)
+    if plan.pair:
+        other = [(i, plan.index_of[(1 - g, c)]) for i, (g, c) in enumerate(plan.place)]
+        arrived.append(lax.ppermute(opening.pop(), "mem", other))
     depth = 3 * (states + 1) * LANES
     analysed = pl.pallas_call(
         functools.partial(analyse_kernel, plan, aligned),
@@ -600,6 +658,8 @@
             pltpu.VMEM((patches, total + 16, depth), bf16),
             pltpu.VMEM((16, depth), f32),
             pltpu.VMEM(side_slot if aligned else (8, LANES), bf16),
+            pltpu.VMEM((total, 2 * states * LANES), bf16),
+            pltpu.VMEM((16, LANES), f32),
         ],
         compiler_params=PARAMS,
         name="analyse",
@@ -630,6 +690,7 @@
         P("mem", "col", None),
         P(),
     )
+
     return jax.shard_map(
         local, mesh=mesh, in_specs=placed, out_specs=P("mem", None, None, "col"), check_vma=False
     )

time: 61.5 us -> 62.5 us (1.016)
  waiting for transfers between devices: 8.72 us -> 12.6 us
  starting transfers between devices: 16.7 us -> 13.8 us
    all_to_all x1, waiting for transfers between devices: 0.01 us -> 4.57 us  [local(): lax.all_to_all(packed, 'mem', split_axis=0, concat_axis=0, tiled=True)]
    ppermute x7 -> x5, starting transfers between devices: 6.63 us -> 3.7 us  [the longest x3 3.55 us: local(): arrived.append(lax.ppermute(parts[k], 'mem', pairing))]
    ppermute x7 -> x5, waiting for transfers between devices: 5.4 us -> 4.75 us  [the longest x3 4.74 us: local(): arrived.append(lax.ppermute(parts[k], 'mem', pairing))]
  transfers between devices with their start and end apart: 10 -> 8, of which waited for: 5 -> 4; matrix products, arithmetic and copies ran while one was open for 0% -> 0% of each run, Pallas kernels for 5% -> 5%
where the time goes in v4:
time: 62.5 us; the launch traced here: 62.1 us
  blocking collectives  17.9 us (29%)
  Pallas kernels  16.4 us (26%)
  starting transfers between devices  13.8 us (22%)
  waiting for transfers between devices  12.6 us (20%)
  local copies, waits for them, and re-layouts  1.25 us (2%)
    all_to_all x1, blocking collectives, local(): lax.all_to_all(analysed, 'mem', split_axis=0, concat_axis=0, tiled=True)  17.9 us
    pallas_call x1, Pallas kernels, local(): pl.pallas_call(functools.partial(analyse_kernel, plan, aligned), out_shap...  7.82 us
    all_to_all x1, starting transfers between devices, local(): lax.all_to_all(packed, 'mem', split_axis=0, concat_axis=0, tiled=True)  5.34 us
    ppermute x3, waiting for transfers between devices, local(): arrived.append(lax.ppermute(parts[k], 'mem', pairing))  4.74 us
    all_to_all x1, waiting for transfers between devices, local(): lax.all_to_all(packed, 'mem', split_axis=0, concat_axis=0, tiled=True)  4.57 us
    ppermute x3, starting transfers between devices, local(): arrived.append(lax.ppermute(parts[k], 'mem', pairing))  3.55 us
    ppermute x1, starting transfers between devices, local(): left = lax.ppermute(upward, 'col', forward)  3.47 us
    ppermute x1, waiting for transfers between devices, local(): right = lax.ppermute(downward, 'col', backward)  3.32 us
  transfers between devices with their start and end apart: 8, of which 4 were waited for; matrix products, arithmetic and copies ran while one was open for 0% of the time, Pallas kernels for 5%

profile of v4, /device:TPU:0, one launch (start us, length us, event | category | flops | bytes accessed | tf_op | source)
XLA Modules:
  0.0 62.1 jit_solution(6318458134175283890)
XLA Ops:
  0.0 0.2 tables.1
  0.2 0.0 copy-start
  0.2 1.2 %copy-done = bf16[32,4,32,128]{3,2,1,0:T(8,128)(2,1)S(1)} copy-done((bf16[32,4,32,128]{3,2,1,0:T(8,128)(2,1)S(1)}, bf16[32,4,32,128]{3,2,1,0:T(8,128)(2,1)}, u32[]{:S(2)}) %copy-start) | copy-done | bytes 1048600
  1.5 2.4 %pack.1 = (bf16[8,16,32,128]{3,2,1,0:T(8,128)(2,1)}, bf16[4,32,32,128]{3,2,1,0:T(8,128)(2,1)S(1)}) custom-call(bf16[32,4,32,128]{3,2,1,0:T(8,128)(2,1)S(1)} %copy-done, bf16[256,256]{1,0:T(8,128)(2,1)S(1)} %get-tuple-element.23.turn_ref, bf16[512,512]{1,0:T(8,128)(2,1)S(1)} %get-tuple-element.24.close_ref), custom_call_target="tpu_custom_call" | custom-call | tf_op jit(solution)/shard_map/pack/pallas_call | solution.py:542
  3.9 0.0 copy-start.5
  3.9 0.0 copy-start.6
  3.9 5.3 %all-to-all-start = ((bf16[8,16,32,128]{3,2,1,0:T(8,128)(2,1)}), bf16[8,16,32,128]{3,2,1,0:T(8,128)(2,1)S(1)}, u32[]{:S(2)}, u32[]{:S(2)}) async-start(bf16[8,16,32,128]{3,2,1,0:T(8,128)(2,1)} %get-tuple-element.25), calls=%async_computation | async-start | bytes 2097152 | tf_op jit(solution)/shard_map/all_to_all | solution.py:555
  9.3 1.0 %sides.1 = (bf16[4,256,128]{2,1,0:T(8,128)(2,1)S(1)}, bf16[256,128]{1,0:T(8,128)(2,1)S(1)}, bf16[256,128]{1,0:T(8,128)(2,1)S(1)}) custom-call(bf16[4,32,32,128]{3,2,1,0:T(8,128)(2,1)S(1)} %get-tuple-element.28.turned), custom_call_target="tpu_custom_call" | custom-call | tf_op jit(solution)/shard_map/sides/pallas_call | solution.py:557
  10.3 3.5 %collective-permute-start = (bf16[256,128]{1,0:T(8,128)(2,1)S(1)}, bf16[256,128]{1,0:T(8,128)(2,1)S(1)}, u32[]{:S(2)}, u32[]{:S(2)}) collective-permute-start(bf16[256,128]{1,0:T(8,128)(2,1)S(1)} %get-tuple-element.30), channel_id=1, source_target_pairs={{0,1},{1,2},{2,3},{4,5},{5,6},{6,7},{8,9},{9,10},{10,11},{12,13},{... | collective-permute-start | bytes 196616 | tf_op jit(solution)/shard_map/ppermute | solution.py:573
  13.7 1.3 %collective-permute-start.1 = (bf16[256,128]{1,0:T(8,128)(2,1)S(1)}, bf16[256,128]{1,0:T(8,128)(2,1)S(1)}, u32[]{:S(2)}, u32[]{:S(2)}) collective-permute-start(bf16[256,128]{1,0:T(8,128)(2,1)S(1)} %get-tuple-element.31), channel_id=1, source_target_pairs={{1,0},{2,1},{3,2},{5,4},{6,5},{7,6},{9,8},{10,9},{11,10},{13,12},{... | collective-permute-start | bytes 196616 | tf_op jit(solution)/shard_map/ppermute | solution.py:574
  15.1 0.0 copy-done.1
  15.1 0.0 copy-done.2
  15.1 0.0 copy-done.3
  15.1 1.5 %maps.1.maps_ref = bf16[4,64,128]{2,1,0:T(8,128)(2,1)S(1)} custom-call(s32[1,4]{1,0:T(1,128)S(1)} %copy-done.5, f32[16]{0:T(128)S(1)} %copy-done.6, s32[4,2048]{1,0:T(4,128)S(1)} %bitcast.5, s32[4,2048]{1,0:T(4,128)S(1)} %bitcast.6, f32[4,2048]{1,0:T(4,128)S(1)} %bitcast.7, f32[4,2048]{1,0:T(4,128)S(1)} %bitcast.8), custom_call_target="tpu_custom_call" | custom-call | tf_op jit(solution)/shard_map/maps/pallas_call | solution.py:576
  16.6 0.0 collective-permute-done.left_ref
  16.6 3.3 %collective-permute-done.1.right_ref = bf16[256,128]{1,0:T(8,128)(2,1)S(1)} collective-permute-done((bf16[256,128]{1,0:T(8,128)(2,1)S(1)}, bf16[256,128]{1,0:T(8,128)(2,1)S(1)}, u32[]{:S(2)}, u32[]{:S(2)}) %collective-permute-start.1) | collective-permute-done | bytes 65568 | tf_op jit(solution)/shard_map/ppermute | solution.py:574
  19.9 0.1 join.1
  20.0 0.1 collective-permute-start.2
  20.1 4.6 %all-to-all-done.x_ref = bf16[8,16,32,128]{3,2,1,0:T(8,128)(2,1)S(1)} async-done(((bf16[8,16,32,128]{3,2,1,0:T(8,128)(2,1)}), bf16[8,16,32,128]{3,2,1,0:T(8,128)(2,1)S(1)}, u32[]{:S(2)}, u32[]{:S(2)}) %all-to-all-start) | async-done | bytes 1048608 | tf_op jit(solution)/shard_map/all_to_all | solution.py:555
  24.7 0.7 %center.1 = (bf16[256,3072]{1,0:T(8,128)(2,1)S(1)}, f32[48,128]{1,0:T(8,128)S(1)}, bf16[256,256]{1,0:T(8,128)(2,1)S(1)}, bf16[512,512]{1,0:T(8,128)(2,1)S(1)}, bf16[8,4,32,128]{3,2,1,0:T(8,128)(2,1)S(1)}) custom-call(s32[1]{0:T(128)} %bitcast.place_ref, bf16[8,16,32,128]{3,2,1,0:T(8,128)(2,1)S(1)} %all-to-all-done.x_ref), custom_call_target="tpu_custom_call" | custom-call | tf_op jit(solution)/shard_map/center/pallas_call | solution.py:633
  25.3 0.1 collective-permute-start.6
  25.4 0.0 collective-permute-done.2.other_ref
  25.5 0.6 collective-permute-start.3
  26.1 0.6 collective-permute-start.4
  26.7 2.3 %collective-permute-start.5 = (bf16[2,7,32,128]{3,2,1,0:T(8,128)(2,1)S(1)}, bf16[2,7,32,128]{3,2,1,0:T(8,128)(2,1)S(1)}, u32[]{:S(2)}, u32[]{:S(2)}) collective-permute-start(bf16[2,7,32,128]{3,2,1,0:T(8,128)(2,1)S(1)} %get-tuple-element.37), channel_id=1, source_target_pairs={{0,24},{4,28},{8,16},{12,20},{16,8},{20,12},{24,0},{28,4},{1,25},{... | collective-permute-start | bytes 344072 | tf_op jit(solution)/shard_map/ppermute | solution.py:615
  29.0 2.5 %collective-permute-done.3.rest_1_ = bf16[2,7,32,128]{3,2,1,0:T(8,128)(2,1)S(1)} collective-permute-done((bf16[2,7,32,128]{3,2,1,0:T(8,128)(2,1)S(1)}, bf16[2,7,32,128]{3,2,1,0:T(8,128)(2,1)S(1)}, u32[]{:S(2)}, u32[]{:S(2)}) %collective-permute-start.3) | collective-permute-done | bytes 114720 | tf_op jit(solution)/shard_map/ppermute | solution.py:615
  31.5 2.2 %collective-permute-done.4.rest_2_ = bf16[2,7,32,128]{3,2,1,0:T(8,128)(2,1)S(1)} collective-permute-done((bf16[2,7,32,128]{3,2,1,0:T(8,128)(2,1)S(1)}, bf16[2,7,32,128]{3,2,1,0:T(8,128)(2,1)S(1)}, u32[]{:S(2)}, u32[]{:S(2)}) %collective-permute-start.4) | collective-permute-done | bytes 114720 | tf_op jit(solution)/shard_map/ppermute | solution.py:615
  33.8 0.0 collective-permute-done.5.rest_3_
  33.8 0.0 collective-permute-done.6.rest_4_
  33.8 7.8 %analyse.1 = bf16[8,16,32,128]{3,2,1,0:T(8,128)(2,1)S(1)} custom-call(s32[1]{0:T(128)} %bitcast.place_ref, bf16[256,3072]{1,0:T(8,128)(2,1)S(1)} %get-tuple-element.26.xs, f32[48,128]{1,0:T(8,128)S(1)} %get-tuple-element.27.avgs, bf16[2,7,32,128]{3,2,1,0:T(8,128)(2,1)S(1)} %get-tuple-element.34.rest_0_, ...), custom_call_target="tpu_custom_call" | custom-call | tf_op jit(solution)/shard_map/analyse/pallas_call | solution.py:650
  41.6 17.9 %all_to_all.10.in_ref = bf16[8,16,32,128]{3,2,1,0:T(8,128)(2,1)S(1)} all-to-all(bf16[8,16,32,128]{3,2,1,0:T(8,128)(2,1)S(1)} %analyse.1), channel_id=1, replica_groups=mesh['mem'=8,'col'=4] {'mem'}, dimensions={0} | all-to-all | bytes 2097152 | tf_op jit(solution)/shard_map/all_to_all | solution.py:669
  59.5 2.6 %unpack.1 = bf16[32,4,32,128]{3,2,1,0:T(8,128)(2,1)} custom-call(bf16[8,16,32,128]{3,2,1,0:T(8,128)(2,1)S(1)} %all_to_all.10.in_ref, bf16[256,256]{1,0:T(8,128)(2,1)S(1)} %get-tuple-element.39.turn_ref, bf16[512,512]{1,0:T(8,128)(2,1)S(1)} %get-tuple-element.40.open_ref), custom_call_target="tpu_custom_call" | custom-call | tf_op jit(solution)/shard_map/unpack/pallas_call | solution.py:672
  (8 shorter events, 0.0 us)
Async XLA Ops:
  0.2 1.2 %copy-start = (bf16[32,4,32,128]{3,2,1,0:T(8,128)(2,1)S(1)}, bf16[32,4,32,128]{3,2,1,0:T(8,128)(2,1)}, u32[]{:S(2)}) copy-start(bf16[32,4,32,128]{3,2,1,0:T(8,128)(2,1)} %x_ref.1) | copy-start | bytes 3145732
  3.9 11.2 %copy-start.1 = (s32[1,4,2048]{2,1,0:T(4,128)S(1)}, s32[1,4,2048]{2,1,0:T(4,128)}, u32[]{:S(2)}) copy-start(s32[1,4,2048]{2,1,0:T(4,128)} %param.9) | copy-start | bytes 98308
  3.9 11.2 %copy-start.2 = (s32[1,4,2048]{2,1,0:T(4,128)S(1)}, s32[1,4,2048]{2,1,0:T(4,128)}, u32[]{:S(2)}) copy-start(s32[1,4,2048]{2,1,0:T(4,128)} %param.10) | copy-start | bytes 98308
  3.9 11.2 %copy-start.3 = (f32[1,4,2048]{2,1,0:T(4,128)S(1)}, f32[1,4,2048]{2,1,0:T(4,128)}, u32[]{:S(2)}) copy-start(f32[1,4,2048]{2,1,0:T(4,128)} %param.11) | copy-start | bytes 98308
  3.9 11.2 %copy-start.4 = (f32[1,4,2048]{2,1,0:T(4,128)S(1)}, f32[1,4,2048]{2,1,0:T(4,128)}, u32[]{:S(2)}) copy-start(f32[1,4,2048]{2,1,0:T(4,128)} %param.12) | copy-start | bytes 98308
  3.9 11.2 %copy-start.5 = (s32[1,4]{1,0:T(1,128)S(1)}, s32[1,4]{1,0:T(1,128)}, u32[]{:S(2)}) copy-start(s32[1,4]{1,0:T(1,128)} %count_ref.1) | copy-start | bytes 52
  3.9 11.2 %copy-start.6 = (f32[16]{0:T(128)S(1)}, f32[16]{0:T(128)}, u32[]{:S(2)}) copy-start(f32[16]{0:T(128)} %factor_ref.1) | copy-start | bytes 196
  3.9 20.7 %all-to-all-start = ((bf16[8,16,32,128]{3,2,1,0:T(8,128)(2,1)}), bf16[8,16,32,128]{3,2,1,0:T(8,128)(2,1)S(1)}, u32[]{:S(2)}, u32[]{:S(2)}) async-start(bf16[8,16,32,128]{3,2,1,0:T(8,128)(2,1)} %get-tuple-element.25), calls=%async_computation | async-start | bytes 2097152 | tf_op jit(solution)/shard_map/all_to_all | solution.py:555
  10.3 6.3 %collective-permute-start = (bf16[256,128]{1,0:T(8,128)(2,1)S(1)}, bf16[256,128]{1,0:T(8,128)(2,1)S(1)}, u32[]{:S(2)}, u32[]{:S(2)}) collective-permute-start(bf16[256,128]{1,0:T(8,128)(2,1)S(1)} %get-tuple-element.30), channel_id=1, source_target_pairs={{0,1},{1,2},{2,3},{4,5},{5,6},{6,7},{8,9},{9,10},{10,11},{12,13},{... | collective-permute-start | bytes 196616 | tf_op jit(solution)/shard_map/ppermute | solution.py:573
  13.7 6.2 %collective-permute-start.1 = (bf16[256,128]{1,0:T(8,128)(2,1)S(1)}, bf16[256,128]{1,0:T(8,128)(2,1)S(1)}, u32[]{:S(2)}, u32[]{:S(2)}) collective-permute-start(bf16[256,128]{1,0:T(8,128)(2,1)S(1)} %get-tuple-element.31), channel_id=1, source_target_pairs={{1,0},{2,1},{3,2},{5,4},{6,5},{7,6},{9,8},{10,9},{11,10},{13,12},{... | collective-permute-start | bytes 196616 | tf_op jit(solution)/shard_map/ppermute | solution.py:574
  20.0 5.4 %collective-permute-start.2 = (bf16[4,7,32,128]{3,2,1,0:T(8,128)(2,1)S(1)}, bf16[4,7,32,128]{3,2,1,0:T(8,128)(2,1)S(1)}, u32[]{:S(2)}, u32[]{:S(2)}) collective-permute-start(bf16[4,7,32,128]{3,2,1,0:T(8,128)(2,1)S(1)} %get-tuple-element.33), channel_id=1, source_target_pairs={{0,4},{4,0},{8,12},{12,8},{16,20},{20,16},{24,28},{28,24},{1,5},{5... | collective-permute-start | bytes 688136 | tf_op jit(solution)/shard_map/ppermute | solution.py:603
  25.3 8.4 %collective-permute-start.6 = (bf16[8,4,32,128]{3,2,1,0:T(8,128)(2,1)S(1)}, bf16[8,4,32,128]{3,2,1,0:T(8,128)(2,1)S(1)}, u32[]{:S(2)}, u32[]{:S(2)}) collective-permute-start(bf16[8,4,32,128]{3,2,1,0:T(8,128)(2,1)S(1)} %get-tuple-element.38), channel_id=1, source_target_pairs={{0,4},{4,0},{8,12},{12,8},{16,20},{20,16},{24,28},{28,24},{1,5},{5... | collective-permute-start | bytes 786440 | tf_op jit(solution)/shard_map/ppermute | solution.py:648
  25.5 6.1 %collective-permute-start.3 = (bf16[2,7,32,128]{3,2,1,0:T(8,128)(2,1)S(1)}, bf16[2,7,32,128]{3,2,1,0:T(8,128)(2,1)S(1)}, u32[]{:S(2)}, u32[]{:S(2)}) collective-permute-start(bf16[2,7,32,128]{3,2,1,0:T(8,128)(2,1)S(1)} %get-tuple-element.35), channel_id=1, source_target_pairs={{0,8},{4,12},{8,0},{12,4},{16,24},{20,28},{24,16},{28,20},{1,9},{5... | collective-permute-start | bytes 344072 | tf_op jit(solution)/shard_map/ppermute | solution.py:615
  26.1 7.7 %collective-permute-start.4 = (bf16[2,7,32,128]{3,2,1,0:T(8,128)(2,1)S(1)}, bf16[2,7,32,128]{3,2,1,0:T(8,128)(2,1)S(1)}, u32[]{:S(2)}, u32[]{:S(2)}) collective-permute-start(bf16[2,7,32,128]{3,2,1,0:T(8,128)(2,1)S(1)} %get-tuple-element.36), channel_id=1, source_target_pairs={{0,16},{4,20},{8,24},{12,28},{16,0},{20,4},{24,8},{28,12},{1,17},{... | collective-permute-start | bytes 344072 | tf_op jit(solution)/shard_map/ppermute | solution.py:615
  26.7 7.1 %collective-permute-start.5 = (bf16[2,7,32,128]{3,2,1,0:T(8,128)(2,1)S(1)}, bf16[2,7,32,128]{3,2,1,0:T(8,128)(2,1)S(1)}, u32[]{:S(2)}, u32[]{:S(2)}) collective-permute-start(bf16[2,7,32,128]{3,2,1,0:T(8,128)(2,1)S(1)} %get-tuple-element.37), channel_id=1, source_target_pairs={{0,24},{4,28},{8,16},{12,20},{16,8},{20,12},{24,0},{28,4},{1,25},{... | collective-permute-start | bytes 344072 | tf_op jit(solution)/shard_map/ppermute | solution.py:615
